TPU v7x, 128 devices: a whole 4x4x4 slice. The times are simulated.
128 devices in a mesh: head: 8 (over x, core), ctx: 16 (over z, y).
Axes of the slice: x: 4, y: 4, z: 4, core: 2. Of those that a mesh axis runs over, the one named last changes fastest.
Arguments:
- query_rows: bfloat16 [16384, 4096], P(('head', 'ctx')), may hold values from -6 to 6
- key_rows: bfloat16 [16384, 4096], P(('head', 'ctx')), may hold values from -6 to 6
- value_rows: bfloat16 [16384, 4096], P(('head', 'ctx')), may hold values from -6 to 6
- token_rates: float32 [16384, 16], P(('head', 'ctx')), may hold values from 0.05 to 0.5
- fast_weights: float32 [16, 3, 1024, 256], P('head'), may hold values from -0.4 to 0.4
- momentum: float32 [16, 3, 1024, 256], P('head'), may hold values from -0.12 to 0.12
- out_weight: bfloat16 [4096, 4096], P('head'), may hold values from -0.09375 to 0.09375
Outputs:
- output: bfloat16 [16384, 4096], P(('head', 'ctx'))
All inputs are finite; a program needn't handle non-finite values.
Results may differ from a plain program's by a relative error of at most 0.035.
Values may be sent and summed in bfloat16 or wider, within the bound.
A program may use at most 128 MiB of HBM per device.

v0:
```python
import jax
import jax.numpy as jnp
from jax import lax
from jax.sharding import PartitionSpec as P


def head_gradient(key_head, value_head, rate_col, weight_bf, rate_scale):
    pre_act = jnp.einsum("td,fd->tf", key_head, weight_bf[0], preferred_element_type=jnp.float32)
    gate_act = jnp.einsum("td,fd->tf", key_head, weight_bf[1], preferred_element_type=jnp.float32)
    sigmoid_pre = jax.nn.sigmoid(pre_act)
    silu_pre = pre_act * sigmoid_pre
    hidden = (silu_pre * gate_act).astype(jnp.bfloat16)
    grad_out = (-(rate_col * rate_scale) * value_head.astype(jnp.float32)).astype(jnp.bfloat16)
    grad_hidden = jnp.einsum(
        "td,fd->tf", grad_out, weight_bf[2], preferred_element_type=jnp.float32
    )
    grad_pre = (
        grad_hidden * gate_act * (sigmoid_pre * (1.0 + pre_act * (1.0 - sigmoid_pre)))
    ).astype(jnp.bfloat16)
    grad_gate = (grad_hidden * silu_pre).astype(jnp.bfloat16)
    return jnp.stack(
        [
            jnp.einsum("tf,td->fd", grad_pre, key_head, preferred_element_type=jnp.float32),
            jnp.einsum("tf,td->fd", grad_gate, key_head, preferred_element_type=jnp.float32),
            jnp.einsum("tf,td->fd", hidden, grad_out, preferred_element_type=jnp.float32),
        ]
    )


def rescale(updated, previous_rows, previous_full, column_new):
    row_old = jnp.sqrt(jnp.sum(jnp.square(previous_rows[:, :2]), axis=3, keepdims=True))
    row_new = jnp.sum(jnp.square(updated[:, :2]), axis=3, keepdims=True)
    first = updated[:, :2] * row_old / jnp.sqrt(row_new + 1e-06)
    column_old = jnp.sqrt(jnp.sum(jnp.square(previous_full[:, 2]), axis=1, keepdims=True))
    second = updated[:, 2] * column_old / jnp.sqrt(column_new + 1e-06)
    return jnp.concatenate([first, second[:, None]], axis=1)


def apply_head(query_head, normed_head):
    pre_act = jnp.einsum(
        "td,fd->tf", query_head, normed_head[0], preferred_element_type=jnp.float32
    )
    gate_act = jnp.einsum(
        "td,fd->tf", query_head, normed_head[1], preferred_element_type=jnp.float32
    )
    hidden = (pre_act * jax.nn.sigmoid(pre_act) * gate_act).astype(jnp.bfloat16)
    return jnp.dot(hidden, normed_head[2], preferred_element_type=jnp.float32).astype(jnp.bfloat16)


def shards(query_rows, key_rows, value_rows, token_rates, fast_weights, momentum, out_weight):
    per_device = fast_weights.shape[0]
    head_width = fast_weights.shape[3]
    group_tokens = key_rows.shape[0] * lax.axis_size("head") * lax.axis_size("ctx")
    rate_scale = float(group_tokens) ** (-0.5)
    query_group, key_group, value_group, rate_group = (
        lax.all_to_all(query_rows, "head", split_axis=1, concat_axis=0, tiled=True),
        lax.all_to_all(key_rows, "head", split_axis=1, concat_axis=0, tiled=True),
        lax.all_to_all(value_rows, "head", split_axis=1, concat_axis=0, tiled=True),
        lax.all_to_all(
            token_rates.astype(jnp.bfloat16), "head", split_axis=1, concat_axis=0, tiled=True
        ).astype(token_rates.dtype),
    )
    gradient_list = []
    for local_head in range(per_device):
        lower = local_head * head_width
        weight_bf = fast_weights[local_head].astype(jnp.bfloat16)
        gradient_list.append(
            head_gradient(
                key_group[:, lower : lower + head_width],
                value_group[:, lower : lower + head_width],
                rate_group[:, local_head : local_head + 1],
                weight_bf,
                rate_scale,
            )
        )
    gradients = jnp.stack(gradient_list)
    summed = lax.psum(gradients.astype(jnp.bfloat16), "ctx").astype(jnp.float32)
    updated = fast_weights - (0.9 * momentum + summed)
    column_new = jnp.sum(jnp.square(updated[:, 2]), axis=1, keepdims=True)
    normed = rescale(updated, fast_weights, fast_weights, column_new).astype(jnp.bfloat16)
    mixed_list = []
    for local_head in range(per_device):
        lower = local_head * head_width
        mixed_list.append(
            apply_head(query_group[:, lower : lower + head_width], normed[local_head])
        )
    mixed = jnp.concatenate(mixed_list, axis=1)
    result = lax.psum_scatter(
        jnp.dot(mixed, out_weight, preferred_element_type=jnp.float32).astype(jnp.bfloat16),
        "head",
        scatter_dimension=0,
        tiled=True,
    )
    return result


def solution(mesh):
    placed = (
        P(("head", "ctx"), None),
        P(("head", "ctx"), None),
        P(("head", "ctx"), None),
        P(("head", "ctx"), None),
        P("head", None, None, None),
        P("head", None, None, None),
        P("head", None),
    )
    return jax.shard_map(
        shards, mesh=mesh, in_specs=placed, out_specs=P(("head", "ctx"), None), check_vma=False
    )
```

profile of v0, /device:TPU:1, one launch (start us, length us, event | category | flops | bytes accessed | tf_op | source)
XLA Modules:
  0.0 270.8 jit_solution(15009734801587680580)
XLA Ops:
  6.5 1.3 convert_element_type.66
  7.8 5.8 %all-to-all-start = ((bf16[128,8,2]{0,2,1:T(2,128)(2,1)}), bf16[128,8,2]{0,2,1:T(2,128)(2,1)S(1)}, u32[]{:S(2)}, u32[]{:S(2)}) async-start(bf16[128,8,2]{0,2,1:T(2,128)(2,1)} %bitcast), calls=%async_computation | async-start | bytes 8192 | tf_op jit(solution)/shard_map/all_to_all | solution.py:59
  13.6 2.3 copy.26
  15.9 2.3 all-to-all-done
  18.2 4.8 %all-to-all-start.2 = ((bf16[128,8,512]{0,2,1:T(8,128)(2,1)}), bf16[128,8,512]{0,2,1:T(8,128)(2,1)}, u32[]{:S(2)}, u32[]{:S(2)}) async-start(bf16[128,8,512]{0,2,1:T(8,128)(2,1)} %bitcast.8), calls=%async_computation.2 | async-start | bytes 2097152 | tf_op jit(solution)/shard_map/all_to_all | solution.py:57
  23.0 3.1 %convert.40 = bf16[2,3,1024,256]{3,2,1,0:T(8,128)(2,1)S(1)} convert(f32[2,3,1024,256]{3,2,1,0:T(8,128)} %param.11) | non-fusion elementwise | flops 1572864 | bytes 9437184 | tf_op jit(solution)/shard_map/convert.21
  26.1 2.2 copy.24
  28.4 9.8 %all-to-all-done.2 = bf16[128,8,512]{0,2,1:T(8,128)(2,1)} async-done(((bf16[128,8,512]{0,2,1:T(8,128)(2,1)}), bf16[128,8,512]{0,2,1:T(8,128)(2,1)}, u32[]{:S(2)}, u32[]{:S(2)}) %all-to-all-start.2) | async-done | bytes 1048608 | tf_op jit(solution)/shard_map/all_to_all | solution.py:57
  38.1 5.1 %all-to-all-start.1 = ((bf16[128,8,512]{0,2,1:T(8,128)(2,1)}), bf16[128,8,512]{0,2,1:T(8,128)(2,1)}, u32[]{:S(2)}, u32[]{:S(2)}) async-start(bf16[128,8,512]{0,2,1:T(8,128)(2,1)} %bitcast.137), calls=%async_computation.1 | async-start | bytes 2097152 | tf_op jit(solution)/shard_map/all_to_all | solution.py:58
  43.2 2.3 copy.27
  45.5 3.8 %fusion.45 = f32[1024,1024]{1,0:T(8,128)} fusion(bf16[2,3,1024,256]{3,2,1,0:T(8,128)(2,1)S(1)} %convert.40, bf16[1024,512]{1,0:T(8,128)(2,1)} %bitcast.121), kind=kOutput, calls=%fused_computation.79 | convolution fusion | flops 536870912 | bytes 5242880 | tf_op jit(solution)/shard_map/td,fd->tf/dot_general | solution.py:9
  49.3 2.7 fusion.44
  52.0 6.3 %all-to-all-done.1 = bf16[128,8,512]{0,2,1:T(8,128)(2,1)} async-done(((bf16[128,8,512]{0,2,1:T(8,128)(2,1)}), bf16[128,8,512]{0,2,1:T(8,128)(2,1)}, u32[]{:S(2)}, u32[]{:S(2)}) %all-to-all-start.1) | async-done | bytes 1048608 | tf_op jit(solution)/shard_map/all_to_all | solution.py:58
  58.3 2.2 copy.25
  60.6 1.9 fusion.46
  62.5 0.4 copy-done.2
  62.9 0.3 copy-done.4
  63.2 3.8 %fusion.29 = bf16[1,1024,256]{2,1,0:T(8,128)(2,1)S(1)} fusion(f32[1024,1024]{1,0:T(8,128)S(1)} %copy-done.2, f32[1024,1024]{1,0:T(8,128)} %fusion.44, bf16[1024,512]{1,0:T(8,128)(2,1)S(1)} %bitcast.134, f32[1024]{0:T(1024)S(1)} %bitcast.142), kind=kOutput, calls=%fused_computation.54 | convolution fusion | flops 544210944 | bytes 9441280 | tf_op jit(solution)/shard_map/tf,td->fd/dot_general | solution.py:25
  67.0 1.6 fusion.28
  68.6 2.2 fusion.26
  70.8 0.7 fusion.42
  71.5 0.7 fusion.41
  72.3 0.8 fusion.43
  73.0 1.4 fusion.31
  74.5 1.6 fusion.30
  76.1 2.2 fusion.27
  78.3 0.6 maximum_bitcast_fusion
  78.8 1.9 pad_maximum_fusion
  80.8 0.0 all-reduce.2.cloned.1.call-update
  80.8 1.3 copy.28
  82.1 4.4 %all-to-all-start.3 = ((bf16[128,8,512]{0,2,1:T(8,128)(2,1)}), bf16[128,8,512]{0,2,1:T(8,128)(2,1)S(1)}, u32[]{:S(2)}, u32[]{:S(2)}) async-start(bf16[128,8,512]{0,2,1:T(8,128)(2,1)} %bitcast.27), calls=%async_computation.3 | async-start | bytes 2097152 | tf_op jit(solution)/shard_map/all_to_all | solution.py:56
  86.6 2.8 %multiply_reduce_fusion.1 = f32[2,2,1024]{2,1,0:T(2,128)S(1)} fusion(f32[2,3,1024,256]{3,2,1,0:T(8,128)} %param.11), kind=kLoop, calls=%fused_computation.18 | loop fusion | flops 2093056 | bytes 4210688 | tf_op jit(solution)/shard_map/reduce_sum | solution.py:31
  89.4 2.2 multiply_reduce_fusion.3
  91.7 9.9 %all-to-all-done.3 = bf16[128,8,512]{0,2,1:T(8,128)(2,1)S(1)} async-done(((bf16[128,8,512]{0,2,1:T(8,128)(2,1)}), bf16[128,8,512]{0,2,1:T(8,128)(2,1)S(1)}, u32[]{:S(2)}, u32[]{:S(2)}) %all-to-all-start.3) | async-done | bytes 1048608 | tf_op jit(solution)/shard_map/all_to_all | solution.py:56
  101.6 0.5 copy.29
  102.1 75.3 %all-reduce.2.cloned.1.call-done = bf16[2,3,1024,256]{3,2,1,0:T(8,128)(2,1)} async-done(((bf16[2,3,1024,256]{3,2,1,0:T(8,128)(2,1)}), bf16[2,3,1024,256]{3,2,1,0:T(8,128)(2,1)}) %all-reduce.2.cloned.1.call-update) | async-done | bytes 3145744 | tf_op jit(solution)/shard_map/psum | solution.py:77
  177.4 6.5 %add_subtract_fusion = f32[2,3,1024,256]{3,2,1,0:T(8,128)S(1)} fusion(f32[2,3,1024,256]{3,2,1,0:T(8,128)} %param.11, bf16[2,3,1024,256]{3,2,1,0:T(8,128)(2,1)} %all-reduce.2.cloned.1.call-done, f32[2,3,1024,256]{3,2,1,0:T(8,128)} %param.12), kind=kLoop, calls=%fused_computation.1 | loop fusion | flops 6291456 | bytes 22020096 | tf_op jit(solution)/shard_map/sub | solution.py:78
  183.9 0.6 multiply_reduce_fusion
  184.6 0.2 multiply_reduce_fusion.2
  184.8 1.4 divide_convert_fusion
  186.2 2.7 fusion.39
  188.9 2.7 fusion.40
  191.5 1.2 divide_convert_fusion.1
  192.7 4.8 %fusion.18 = bf16[1024,256]{0,1:T(8,128)(2,1)} fusion(f32[1024,1024]{0,1:T(8,128)} %fusion.39, bf16[2,1,1024,256]{3,2,1,0:T(8,128)(2,1)} %divide_convert_fusion.1, bf16[2,2,1024,256]{3,2,1,0:T(8,128)(2,1)S(1)} %divide_convert_fusion, bf16[1024,512]{1,0:T(8,128)(2,1)S(1)} %bitcast.131), kind=kOutput, calls=%fused_computation.43 | convolution fusion | flops 1080295424 | bytes 6291456 | tf_op jit(solution)/shard_map/dot_general | solution.py:47
  197.6 4.8 %fusion.19 = bf16[1024,256]{0,1:T(8,128)(2,1)} fusion(f32[1024,1024]{0,1:T(8,128)} %fusion.40, bf16[2,1,1024,256]{3,2,1,0:T(8,128)(2,1)} %divide_convert_fusion.1, bf16[2,2,1024,256]{3,2,1,0:T(8,128)(2,1)S(1)} %divide_convert_fusion, bf16[1024,512]{1,0:T(8,128)(2,1)S(1)} %bitcast.132), kind=kOutput, calls=%fused_computation.44 | convolution fusion | flops 1080295424 | bytes 6291456 | tf_op jit(solution)/shard_map/dot_general | solution.py:47
  202.4 10.3 %convolution_convert_fusion = bf16[1024,4096]{1,0:T(8,128)(2,1)} fusion(bf16[512,4096]{1,0:T(8,128)(2,1)} %param.13, bf16[1024,256]{0,1:T(8,128)(2,1)} %fusion.18, bf16[1024,256]{0,1:T(8,128)(2,1)} %fusion.19), kind=kOutput, calls=%fused_computation | convolution fusion | flops 4301258752 | bytes 13631488 | tf_op jit(solution)/shard_map/dot_general | solution.py:89
  212.7 0.0 reduce-scatter.2.cloned.1.call-update
  212.7 51.2 %reduce-scatter.2.cloned.1.call-done = bf16[128,4096]{1,0:T(8,128)(2,1)} async-done(((bf16[1024,4096]{1,0:T(8,128)(2,1)}), bf16[128,4096]{1,0:T(8,128)(2,1)}) %reduce-scatter.2.cloned.1.call-update) | async-done | bytes 1048592 | tf_op jit(solution)/shard_map/reduce_scatter | solution.py:88
  (18 shorter events, 0.1 us)
Async XLA Ops:
  7.8 10.4 %all-to-all-start = ((bf16[128,8,2]{0,2,1:T(2,128)(2,1)}), bf16[128,8,2]{0,2,1:T(2,128)(2,1)S(1)}, u32[]{:S(2)}, u32[]{:S(2)}) async-start(bf16[128,8,2]{0,2,1:T(2,128)(2,1)} %bitcast), calls=%async_computation | async-start | bytes 8192 | tf_op jit(solution)/shard_map/all_to_all | solution.py:59
  18.2 19.9 %all-to-all-start.2 = ((bf16[128,8,512]{0,2,1:T(8,128)(2,1)}), bf16[128,8,512]{0,2,1:T(8,128)(2,1)}, u32[]{:S(2)}, u32[]{:S(2)}) async-start(bf16[128,8,512]{0,2,1:T(8,128)(2,1)} %bitcast.8), calls=%async_computation.2 | async-start | bytes 2097152 | tf_op jit(solution)/shard_map/all_to_all | solution.py:57
  38.1 20.2 %all-to-all-start.1 = ((bf16[128,8,512]{0,2,1:T(8,128)(2,1)}), bf16[128,8,512]{0,2,1:T(8,128)(2,1)}, u32[]{:S(2)}, u32[]{:S(2)}) async-start(bf16[128,8,512]{0,2,1:T(8,128)(2,1)} %bitcast.137), calls=%async_computation.1 | async-start | bytes 2097152 | tf_op jit(solution)/shard_map/all_to_all | solution.py:58
  43.2 134.2 %all-reduce.2.cloned.1.call-start = ((), (), s32[]{:S(2)}) async-start(), calls=%async_computation.5 | async-start | bytes 6291456 | tf_op jit(solution)/shard_map/psum | solution.py:77
  45.5 3.8 %copy-start = (bf16[8,128,512]{2,1,0:T(8,128)(2,1)S(1)}, bf16[8,128,512]{2,1,0:T(8,128)(2,1)}, u32[]{:S(2)}) copy-start(bf16[8,128,512]{2,1,0:T(8,128)(2,1)} %copy.27) | copy-start | bytes 3145732
  60.6 2.3 copy-start.2
  60.6 2.6 copy-start.4
  63.2 3.8 %copy-start.1 = (bf16[8,128,512]{2,1,0:T(8,128)(2,1)S(1)}, bf16[8,128,512]{2,1,0:T(8,128)(2,1)}, u32[]{:S(2)}) copy-start(bf16[8,128,512]{2,1,0:T(8,128)(2,1)} %copy.27) | copy-start | bytes 3145732
  63.2 3.8 %copy-start.3 = (f32[1024,1024]{1,0:T(8,128)S(1)}, f32[1024,1024]{1,0:T(8,128)}, u32[]{:S(2)}) copy-start(f32[1024,1024]{1,0:T(8,128)} %fusion.44) | copy-start | bytes 12582916
  78.8 2.0 copy-start.5
  82.1 19.4 %all-to-all-start.3 = ((bf16[128,8,512]{0,2,1:T(8,128)(2,1)}), bf16[128,8,512]{0,2,1:T(8,128)(2,1)S(1)}, u32[]{:S(2)}, u32[]{:S(2)}) async-start(bf16[128,8,512]{0,2,1:T(8,128)(2,1)} %bitcast.27), calls=%async_computation.3 | async-start | bytes 2097152 | tf_op jit(solution)/shard_map/all_to_all | solution.py:56
  86.6 177.4 %reduce-scatter.2.cloned.1.call-start = ((), (), s32[]{:S(2)}) async-start(), calls=%async_computation.6 | async-start | bytes 9437184 | tf_op jit(solution)/shard_map/reduce_scatter | solution.py:88
Sparse Core Ops, SparseCore 0:
  80.9 96.4 all-reduce.1
  212.8 51.0 reduce-scatter.1
where the time goes:
time: 271 us
  waiting for transfers between devices  155 us (57%)
  matrix products  48.8 us (18%)
  other arithmetic  21.9 us (8%)
  starting transfers between devices  20.1 us (7%)
  between operations  13.6 us (5%)
  local copies, waits for them, and re-layouts  11.6 us (4%)
    psum x1, waiting for transfers between devices, shards(): summed = lax.psum(gradients.astype(jnp.bfloat16), 'ctx').astype(jnp.float32)  75.3 us
    reduce_scatter x1, waiting for transfers between devices, shards(): lax.psum_scatter(jnp.dot(mixed, out_weight, preferred_element_type=jnp.fl...  51.2 us
    dot_general x1, matrix products, shards(): jnp.dot(mixed, out_weight, preferred_element_type=jnp.float32)  10.3 us
    all_to_all x1, waiting for transfers between devices, shards(): lax.all_to_all(query_rows, 'head', split_axis=1, concat_axis=0, tiled=True)  9.9 us
    all_to_all x1, waiting for transfers between devices, shards(): lax.all_to_all(key_rows, 'head', split_axis=1, concat_axis=0, tiled=True)  9.76 us
    dot_general x2, matrix products, apply_head(): jnp.dot(hidden, normed_head[2], preferred_element_type=jnp.float32)  9.65 us
    sub x1, other arithmetic, shards(): updated = fast_weights - (0.9 * momentum + summed)  6.55 us
    unnamed x15, local copies, waits for them, and re-layouts  6.53 us
  transfers between devices with their start and end apart: 6, of which 6 were waited for; matrix products, arithmetic and copies ran while one was open for 9% of the time, Pallas kernels for 0%

commit v1 on v0

v1 whole, which is shorter than its diff:
```python
import functools

import jax
import jax.numpy as jnp
from jax import lax
from jax.experimental import pallas as pl
from jax.experimental.pallas import tpu as pltpu
from jax.sharding import PartitionSpec as P

MESH = pl.DeviceIdType.MESH
F32 = jnp.float32
BF16 = jnp.bfloat16

OFFSETS = (
    (0, 0), (0, 1), (0, 3), (0, 2),
    (1, 0), (1, 1), (1, 3), (1, 2),
    (3, 0), (3, 1), (3, 3), (3, 2),
    (2, 0), (2, 1), (2, 3), (2, 2),
)
SEND_ORDER = (1, 4, 8, 2, 12, 3, 5, 9, 6, 10, 13, 14, 7, 11, 15)
NT = (((1,), (1,)), ((), ()))


def dot_nt(a, b):
    return lax.dot_general(a, b, NT, preferred_element_type=F32)


def dot_nn(a, b):
    return jnp.dot(a, b, preferred_element_type=F32)


def kernel(
    rate_scale,
    q_ref, k_ref, v_ref, rates_ref, fast_ref, mom_ref, wout_ref,
    out_ref,
    gsrc, kbuf, gbuf, qbuf, wf, wb, mom, grad,
    csend, crecv, zsend, zrecv, normed, cscale,
    osend, obuf, wout, stash, total, msend, mrecv,
    a2a_send, a2a_recv, loc_sem, w_send, w_recv, cs_sem, cr_sem, zs_sem, zr_sem,
    ns_sem, nr_sem, ps_sem, pr_sem, os_sem, or_sem, ms_sem, mr_sem, wo_send, wo_recv,
):
    head, ctx = lax.axis_index("head"), lax.axis_index("ctx")
    x, c = head // 2, head % 2
    z, y = ctx // 4, ctx % 4
    owner = y // 2
    local = y % 2

    def dev(dx=0, dy=0, dz=0, dc=0):
        return (((x + dx) % 4) * 2 + (c + dc) % 2, ((z + dz) % 4) * 4 + (y + dy) % 4)

    def remote(src, dst, ssem, rsem, where):
        return pltpu.make_async_remote_copy(
            src_ref=src, dst_ref=dst, send_sem=ssem, recv_sem=rsem, device_id=where, device_id_type=MESH
        )

    barrier = pltpu.get_barrier_semaphore()
    for dx, dy in OFFSETS[1:]:
        pl.semaphore_signal(barrier, inc=1, device_id=dev(dx, dy), device_id_type=MESH)
    for dz in (1, 2, 3):
        pl.semaphore_signal(barrier, inc=1, device_id=dev(dz=dz), device_id_type=MESH)
    pl.semaphore_signal(barrier, inc=1, device_id=dev(dc=1), device_id_type=MESH)

    for h in range(16):
        cols = pl.ds(h * 256, 256)
        gsrc[:, cols] = (-(rates_ref[:, h : h + 1] * rate_scale) * v_ref[:, cols].astype(F32)).astype(BF16)

    mine = pl.multiple_of((x * 4 + y) * 256, 256)
    k_own = pltpu.make_async_copy(k_ref.at[:, pl.ds(mine, 256)], kbuf.at[pl.ds(0, 128)], a2a_recv.at[0, 0])
    q_own = pltpu.make_async_copy(q_ref.at[:, pl.ds(mine, 256)], qbuf.at[pl.ds(0, 128)], a2a_recv.at[2, 0])
    k_own.start()
    gbuf[pl.ds(0, 128), :] = gsrc[:, pl.ds(mine, 256)]

    pl.semaphore_wait(barrier, 19)

    def block_copy(kind, source, target, slot):
        dx, dy = OFFSETS[slot]
        to = pl.multiple_of((((x + dx) % 4) * 4 + (y + dy) % 4) * 256, 256)
        return remote(
            source.at[:, pl.ds(to, 256)], target.at[pl.ds(slot * 128, 128)],
            a2a_send.at[kind, slot], a2a_recv.at[kind, slot], dev(dx, dy),
        )

    def weights_in(m):
        return pltpu.make_async_copy(fast_ref.at[local, m], wf.at[m], loc_sem.at[m])

    def weights_over(m):
        return remote(fast_ref.at[local, m], wf.at[m], w_send.at[m], w_recv.at[m], dev(dc=1))

    row_own = pl.multiple_of(c * 512 + z * 128, 128)
    row_other = pl.multiple_of((1 - c) * 512 + z * 128, 128)
    mom_in = pltpu.make_async_copy(mom_ref.at[local, :, pl.ds(row_own, 128)], mom, loc_sem.at[3])
    mom_over = remote(mom_ref.at[local, :, pl.ds(row_other, 128)], mom, w_send.at[3], w_recv.at[3], dev(dc=1))

    a2a = []
    for slot in SEND_ORDER[:3]:
        for kind, source, target in ((0, k_ref, kbuf), (1, gsrc, gbuf)):
            copy = block_copy(kind, source, target, slot)
            copy.start()
            a2a.append(copy)

    @pl.when(c == owner)
    def _():
        for m in range(3):
            weights_over(m).start()
            weights_in(m).start()
        mom_over.start()
        mom_in.start()

    for slot in SEND_ORDER[3:]:
        for kind, source, target in ((0, k_ref, kbuf), (1, gsrc, gbuf)):
            copy = block_copy(kind, source, target, slot)
            copy.start()
            a2a.append(copy)
    for slot in SEND_ORDER:
        copy = block_copy(2, q_ref, qbuf, slot)
        copy.start()
        a2a.append(copy)
    q_own.start()

    for m in range(3):
        @pl.when(c == owner)
        def _():
            weights_in(m).wait()

        @pl.when(c != owner)
        def _():
            weights_over(m).wait_recv()

        wb[m] = wf[m].astype(BF16)

    chunk = 512

    def grad_block(t, first):
        toks = pl.ds(pl.multiple_of(t * 256, 256), 256)

        def body(i, carry):
            rows = pl.ds(pl.multiple_of(i * chunk, chunk), chunk)
            keys, gout = kbuf[toks, :], gbuf[toks, :]
            pre = dot_nt(wb[0, rows, :], keys)
            gate = dot_nt(wb[1, rows, :], keys)
            back = dot_nt(wb[2, rows, :], gout)
            sg = 0.5 + 0.5 * jnp.tanh(0.5 * pre)
            silu = pre * sg
            hidden = (silu * gate).astype(BF16)
            grad_gate = (back * silu).astype(BF16)
            grad_pre = ((back * gate) * (sg + silu - silu * sg)).astype(BF16)
            g0 = dot_nn(grad_pre, keys)
            g1 = dot_nn(grad_gate, keys)
            g2 = dot_nn(hidden, gout)
            if first:
                grad[0, rows, :] = g0
                grad[1, rows, :] = g1
                grad[2, rows, :] = g2
            else:
                grad[0, rows, :] += g0
                grad[1, rows, :] += g1
                grad[2, rows, :] += g2
            return carry

        lax.fori_loop(0, 1024 // chunk, body, 0)

    def slot_wait(kind, target, slot):
        remote(
            target.at[pl.ds(0, 128)], target.at[pl.ds(slot * 128, 128)],
            a2a_send.at[kind, slot], a2a_recv.at[kind, slot], dev(1),
        ).wait_recv()

    k_own.wait()
    slot_wait(0, kbuf, 1)
    slot_wait(1, gbuf, 1)
    grad_block(0, True)

    def later(t, carry):
        for j in range(2):
            slot = 2 * t + j
            slot_wait(0, kbuf, slot)
            slot_wait(1, gbuf, slot)
        grad_block(t, False)
        return carry

    lax.fori_loop(1, 8, later, 0)

    wo_rows = pl.ds(pl.multiple_of(c * 512, 512), 512)
    wo_in = pltpu.make_async_copy(wout_ref, wout.at[wo_rows], loc_sem.at[4])
    wo_over = remote(wout_ref, wout.at[wo_rows], wo_send, wo_recv, dev(dc=1))

    core_copies = []
    for n, dz in enumerate((2, 1, 3, 0)):
        rows = pl.ds(pl.multiple_of((1 - c) * 512 + ((z + dz) % 4) * 128, 128), 128)
        csend[n] = grad[:, rows, :].astype(BF16)
        copy = remote(csend.at[n], crecv.at[n], cs_sem.at[n], cr_sem.at[n], dev(dc=1))
        copy.start()
        core_copies.append(copy)
    z_copies = []
    for n, dz in enumerate((2, 1, 3)):
        rows = pl.ds(pl.multiple_of(c * 512 + ((z + dz) % 4) * 128, 128), 128)
        core_copies[n].wait_recv()
        zsend[n] = (grad[:, rows, :] + crecv[n].astype(F32)).astype(BF16)
        copy = remote(zsend.at[n], zrecv.at[n], zs_sem.at[n], zr_sem.at[n], dev(dz=dz))
        copy.start()
        z_copies.append(copy)
    wo_in.start()
    wo_over.start()
    core_copies[3].wait_recv()
    own = pl.ds(row_own, 128)

    @pl.when(c == owner)
    def _():
        mom_in.wait()

    @pl.when(c != owner)
    def _():
        mom_over.wait_recv()

    base = wf[:, own, :] - 0.9 * mom[...] - (grad[:, own, :] + crecv[3].astype(F32))
    grad[:, own, :] = base
    row_old = jnp.sqrt(jnp.sum(jnp.square(wf[0:2, own, :]), axis=2, keepdims=True))
    column_old = jnp.sqrt(jnp.sum(jnp.square(wf[2]), axis=0, keepdims=True))
    for n in range(3):
        z_copies[n].wait_recv()
    updated = grad[:, own, :] - (zrecv[0].astype(F32) + zrecv[1].astype(F32) + zrecv[2].astype(F32))
    row_new = jnp.sum(jnp.square(updated[0:2]), axis=2, keepdims=True)
    normed[0:2, own, :] = (updated[0:2] * row_old / jnp.sqrt(row_new + 1e-06)).astype(BF16)
    normed[2, own, :] = updated[2].astype(BF16)

    n_copies, p_copies = [], []
    for n, dz in enumerate((2, 1, 3)):
        copy = remote(normed.at[:, own], normed.at[:, own], ns_sem.at[n], nr_sem.at[n], dev(dz=dz))
        copy.start()
        n_copies.append(copy)
    copy = remote(normed.at[:, own], normed.at[:, own], ps_sem.at[3], pr_sem.at[3], dev(dc=1))
    copy.start()
    p_copies.append(copy)
    for n, dz in ((1, 1), (2, 3), (0, 2)):
        n_copies[n].wait_recv()
        rows = pl.ds(pl.multiple_of(c * 512 + ((z - dz) % 4) * 128, 128), 128)
        copy = remote(normed.at[:, rows], normed.at[:, rows], ps_sem.at[n], pr_sem.at[n], dev(dc=1))
        copy.start()
        p_copies.append(copy)
    for copy in p_copies:
        copy.wait_recv()
    column_new = jnp.sum(jnp.square(normed[2].astype(F32)), axis=0, keepdims=True)
    cscale[...] = column_old / jnp.sqrt(column_new + 1e-06)

    q_own.wait()

    def apply_slots(t):
        toks = pl.ds(t * 256, 256)

        def body(i, acc):
            rows = pl.ds(pl.multiple_of(i * chunk, chunk), chunk)
            query = qbuf[toks, :]
            pre = dot_nt(query, normed[0, rows, :])
            gate = dot_nt(query, normed[1, rows, :])
            hidden = (pre * (0.5 + 0.5 * jnp.tanh(0.5 * pre)) * gate).astype(BF16)
            return acc + dot_nn(hidden, normed[2, rows, :])

        acc = lax.fori_loop(0, 1024 // chunk, body, jnp.zeros((256, 256), F32))
        osend[toks, :] = (acc * cscale[...]).astype(BF16)

    my_cols = pl.ds(pl.multiple_of(y * 256, 256), 256)
    o_copies = []
    for t in (6, 7, 4, 5, 2, 3, 0, 1):
        for slot in (2 * t, 2 * t + 1):
            if slot > 0:
                slot_wait(2, qbuf, slot)
        apply_slots(t)
        for slot in (2 * t, 2 * t + 1):
            dx, dy = OFFSETS[slot]
            if dy == 0:
                obuf[pl.ds(dx * 128, 128), my_cols] = osend[pl.ds(slot * 128, 128), :]
            else:
                copy = remote(
                    osend.at[pl.ds(slot * 128, 128)], obuf.at[pl.ds(dx * 128, 128), my_cols],
                    os_sem.at[dx, dy], or_sem.at[dx, dy], dev(dy=-dy),
                )
                copy.start()
                o_copies.append(copy)

    wo_in.wait()
    wo_over.wait_recv()

    def o_wait(dx):
        for dy in (1, 2, 3):
            remote(
                osend.at[pl.ds(0, 128)], obuf.at[pl.ds(dx * 128, 128), pl.ds(0, 256)],
                os_sem.at[dx, dy], or_sem.at[dx, dy], dev(1),
            ).wait_recv()

    def message(kind, j, up):
        return remote(
            msend.at[kind, j], mrecv.at[kind, j], ms_sem.at[kind, j], mr_sem.at[kind, j], dev(1 if up else -1)
        )

    def product(first, rows, j):
        return dot_nn(obuf[pl.ds(first, rows), :], wout[:, pl.ds(pl.multiple_of(j * 512, 512), 512)])

    o_wait(2)

    def far(j, carry):
        msend[0, j] = product(256, 128, j).astype(BF16)
        message(0, j, True).start()
        msend[1, j] = product(256, 128, j + 4).astype(BF16)
        message(1, j, False).start()
        return carry

    lax.fori_loop(0, 4, far, 0)
    o_wait(1)
    o_wait(3)

    def near(j, carry):
        msend[2, j] = product(384, 128, j + 4).astype(BF16)
        message(2, j, True).start()
        msend[3, j] = product(128, 128, j).astype(BF16)
        message(3, j, False).start()
        return carry

    lax.fori_loop(0, 4, near, 0)

    def relay_part(j, carry):
        stash[0, j] = product(384, 128, j)
        stash[1, j] = product(128, 128, j + 4)
        return carry

    lax.fori_loop(0, 4, relay_part, 0)

    def relay(j, carry):
        message(0, j, True).wait_recv()
        msend[4, j] = (stash[0, j] + mrecv[0, j].astype(F32)).astype(BF16)
        message(4, j, True).start()
        message(1, j, False).wait_recv()
        msend[5, j] = (stash[1, j] + mrecv[1, j].astype(F32)).astype(BF16)
        message(5, j, False).start()
        return carry

    lax.fori_loop(0, 4, relay, 0)
    o_wait(0)

    def rest(j, carry):
        total[j] = product(0, 128, j)
        return carry

    lax.fori_loop(0, 8, rest, 0)

    def finish(j, carry):
        low = pl.ds(pl.multiple_of(j * 512, 512), 512)
        high = pl.ds(pl.multiple_of(j * 512 + 2048, 512), 512)
        message(3, j, False).wait_recv()
        message(2, j, True).wait_recv()
        message(4, j, True).wait_recv()
        out_ref[:, low] = (total[j] + mrecv[3, j].astype(F32) + mrecv[4, j].astype(F32)).astype(BF16)
        message(5, j, False).wait_recv()
        out_ref[:, high] = (total[j + 4] + mrecv[2, j].astype(F32) + mrecv[5, j].astype(F32)).astype(BF16)
        return carry

    lax.fori_loop(0, 4, finish, 0)

    for copy in a2a + core_copies + z_copies + n_copies + p_copies + o_copies:
        copy.wait_send()
    wo_over.wait_send()

    @pl.when(c == owner)
    def _():
        for m in range(3):
            weights_over(m).wait_send()
        mom_over.wait_send()

    def drain(j, carry):
        for kind in range(6):
            message(kind, j, kind % 2 == 0).wait_send()
        return carry

    lax.fori_loop(0, 4, drain, 0)


def shards(query_rows, key_rows, value_rows, token_rates, fast_weights, momentum, out_weight):
    tokens = key_rows.shape[0] * lax.axis_size("head") * lax.axis_size("ctx")
    anywhere = pl.BlockSpec(memory_space=pl.ANY)
    vmem = pl.BlockSpec(memory_space=pltpu.VMEM)
    dma = pltpu.SemaphoreType.DMA
    return pl.pallas_call(
        functools.partial(kernel, float(tokens) ** (-0.5)),
        out_shape=jax.ShapeDtypeStruct((128, 4096), BF16),
        in_specs=[anywhere, anywhere, vmem, vmem, anywhere, anywhere, anywhere],
        out_specs=vmem,
        scratch_shapes=[
            pltpu.VMEM((128, 4096), BF16),
            pltpu.VMEM((2048, 256), BF16),
            pltpu.VMEM((2048, 256), BF16),
            pltpu.VMEM((2048, 256), BF16),
            pltpu.VMEM((3, 1024, 256), F32),
            pltpu.VMEM((3, 1024, 256), BF16),
            pltpu.VMEM((3, 128, 256), F32),
            pltpu.VMEM((3, 1024, 256), F32),
            pltpu.VMEM((4, 3, 128, 256), BF16),
            pltpu.VMEM((4, 3, 128, 256), BF16),
            pltpu.VMEM((3, 3, 128, 256), BF16),
            pltpu.VMEM((3, 3, 128, 256), BF16),
            pltpu.VMEM((3, 1024, 256), BF16),
            pltpu.VMEM((1, 256), F32),
            pltpu.VMEM((2048, 256), BF16),
            pltpu.VMEM((512, 1024), BF16),
            pltpu.VMEM((1024, 4096), BF16),
            pltpu.VMEM((2, 4, 128, 512), F32),
            pltpu.VMEM((8, 128, 512), F32),
            pltpu.VMEM((6, 4, 128, 512), BF16),
            pltpu.VMEM((6, 4, 128, 512), BF16),
            dma((3, 16)), dma((3, 16)), dma((5,)), dma((4,)), dma((4,)), dma((4,)), dma((4,)), dma((3,)), dma((3,)),
            dma((3,)), dma((3,)), dma((4,)), dma((4,)), dma((4, 4)), dma((4, 4)), dma((6, 4)), dma((6, 4)), dma(()), dma(()),
        ],
        compiler_params=pltpu.CompilerParams(collective_id=0, has_side_effects=True, vmem_limit_bytes=62 * 2**20),
        name="ttt_layer",
    )(query_rows, key_rows, value_rows, token_rates, fast_weights, momentum, out_weight)


def solution(mesh):
    placed = (
        P(("head", "ctx"), None),
        P(("head", "ctx"), None),
        P(("head", "ctx"), None),
        P(("head", "ctx"), None),
        P("head", None, None, None),
        P("head", None, None, None),
        P("head", None),
    )
    return jax.shard_map(
        shards, mesh=mesh, in_specs=placed, out_specs=P(("head", "ctx"), None), check_vma=False
    )
```

time: 271 us -> 121 us (0.45)
  waiting for transfers between devices: 155 us -> 0 us
  Pallas kernels: 0 us -> 116 us
  matrix products: 48.8 us -> 0 us
  other arithmetic: 21.9 us -> 0 us
  starting transfers between devices: 20.1 us -> 0 us
  between operations: 13.6 us -> 0.01 us
  local copies, waits for them, and re-layouts: 11.6 us -> 3.71 us
    pallas_call x0 -> x1, Pallas kernels: none -> 116 us  [shards(): pl.pallas_call(functools.partial(kernel, float(tokens) ** (-0.5)), out_sh...]
    psum x1 -> x0, waiting for transfers between devices: 75.3 us -> none  [shards(): summed = lax.psum(gradients.astype(jnp.bfloat16), 'ctx').astype(jnp.float32)]
    reduce_scatter x1 -> x0, waiting for transfers between devices: 51.2 us -> none  [shards(): lax.psum_scatter(jnp.dot(mixed, out_weight, preferred_element_type=jnp.fl...]
    dot_general x17 -> x0, matrix products: 48.8 us -> none  [the longest x1 10.3 us: shards(): jnp.dot(mixed, out_weight, preferred_element_type=jnp.float32)]
    all_to_all x4 -> x0, waiting for transfers between devices: 28.3 us -> none  [the longest x1 9.9 us: shards(): lax.all_to_all(query_rows, 'head', split_axis=1, concat_axis=0, tiled=True)]
    all_to_all x4 -> x0, starting transfers between devices: 20.1 us -> none  [the longest x1 5.79 us: shards(): lax.all_to_all(token_rates.astype(jnp.bfloat16), 'head', split_axis=1, co...]
    another operation x5 -> x0, other arithmetic: 8.13 us -> none
    sub x1 -> x0, other arithmetic: 6.55 us -> none  [shards(): updated = fast_weights - (0.9 * momentum + summed)]
  transfers between devices with their start and end apart: 6 -> 0, of which waited for: 6 -> 0; matrix products, arithmetic and copies ran while one was open for 9% -> 0% of each run, Pallas kernels for 0% -> 0%
where the time goes in v1:
time: 121 us; the launch traced here: 120 us
  Pallas kernels  116 us (96%)
  local copies, waits for them, and re-layouts  3.71 us (3%)
    pallas_call x1, Pallas kernels, shards(): pl.pallas_call(functools.partial(kernel, float(tokens) ** (-0.5)), out_sh...  116 us
    unnamed x2, local copies, waits for them, and re-layouts  3.71 us

profile of v1, /device:TPU:1, one launch (start us, length us, event | category | flops | bytes accessed | tf_op | source)
XLA Modules:
  0.0 119.6 jit_solution(12136056329248388314)
XLA Ops:
  0.0 1.4 %copy.8.rates_ref = f32[128,16]{1,0:T(8,128)} copy(f32[128,16]{0,1:T(8,128)} %param.10) | data formatting | bytes 16384 | tf_op args[3]
  1.4 115.9 %ttt_layer.1 = bf16[128,4096]{1,0:T(8,128)(2,1)} custom-call(bf16[128,4096]{1,0:T(8,128)(2,1)} %q_ref.1, bf16[128,4096]{1,0:T(8,128)(2,1)} %k_ref.1, bf16[128,4096]{1,0:T(8,128)(2,1)} %v_ref.1, f32[128,16]{1,0:T(8,128)} %copy.8.rates_ref, f32[2,3,1024,256]{3,2,1,0:T(8,128)} %fast_ref.1, f32[2,3,1024,256]{3,2,1,0:T(8,128)} %mom_ref.1, bf16[512,4096]{1,0:T(8,128)(2,1)} %wout_ref.1), custom_call_target="tpu_custom_call" | custom-call | tf_op jit(solution)/shard_map/ttt_layer/pallas_call | solution.py:381
  117.3 2.3 %copy.10 = bf16[128,4096]{1,0:T(8,128)(2,1)} copy(bf16[128,4096]{1,0:T(8,128)(2,1)} %ttt_layer.1) | data formatting | bytes 2097152

commit v2 on v1

--- a/solution.py
+++ b/solution.py
@@ -11,13 +11,21 @@
 F32 = jnp.float32
 BF16 = jnp.bfloat16
 
-OFFSETS = (
+K_OFFSETS = (
+    (0, 0), (2, 2), (1, 1), (3, 3),
+    (2, 1), (1, 2), (2, 3), (3, 2),
+    (2, 0), (0, 2), (1, 3), (3, 1),
+    (1, 0), (0, 1), (3, 0), (0, 3),
+)
+Q_OFFSETS = (
     (0, 0), (0, 1), (0, 3), (0, 2),
-    (1, 0), (1, 1), (1, 3), (1, 2),
-    (3, 0), (3, 1), (3, 3), (3, 2),
     (2, 0), (2, 1), (2, 3), (2, 2),
+    (1, 2), (3, 2), (1, 1), (3, 3),
+    (1, 3), (3, 1), (1, 0), (3, 0),
 )
-SEND_ORDER = (1, 4, 8, 2, 12, 3, 5, 9, 6, 10, 13, 14, 7, 11, 15)
+Q_ORDER = (7, 10, 11, 5, 8, 6, 9, 4, 3, 12, 13, 14, 1, 15, 2)
+
+
 NT = (((1,), (1,)), ((), ()))
 
 
@@ -35,9 +43,9 @@
     out_ref,
     gsrc, kbuf, gbuf, qbuf, wf, wb, mom, grad,
     csend, crecv, zsend, zrecv, normed, cscale,
-    osend, obuf, wout, stash, total, msend, mrecv,
+    osend, obuf, wout, stash, total, msend, mrecv, fsend, frecv,
     a2a_send, a2a_recv, loc_sem, w_send, w_recv, cs_sem, cr_sem, zs_sem, zr_sem,
-    ns_sem, nr_sem, ps_sem, pr_sem, os_sem, or_sem, ms_sem, mr_sem, wo_send, wo_recv,
+    ns_sem, nr_sem, ps_sem, pr_sem, os_sem, or_sem, ms_sem, mr_sem, fs_sem, fr_sem, wo_send, wo_recv,
 ):
     head, ctx = lax.axis_index("head"), lax.axis_index("ctx")
     x, c = head // 2, head % 2
@@ -54,15 +62,16 @@
         )
 
     barrier = pltpu.get_barrier_semaphore()
-    for dx, dy in OFFSETS[1:]:
+    for dx, dy in K_OFFSETS[1:]:
         pl.semaphore_signal(barrier, inc=1, device_id=dev(dx, dy), device_id_type=MESH)
     for dz in (1, 2, 3):
         pl.semaphore_signal(barrier, inc=1, device_id=dev(dz=dz), device_id_type=MESH)
     pl.semaphore_signal(barrier, inc=1, device_id=dev(dc=1), device_id_type=MESH)
 
+    scaled = -(rates_ref[...].T * rate_scale)
     for h in range(16):
         cols = pl.ds(h * 256, 256)
-        gsrc[:, cols] = (-(rates_ref[:, h : h + 1] * rate_scale) * v_ref[:, cols].astype(F32)).astype(BF16)
+        gsrc[:, cols] = (scaled[:, h : h + 1] * v_ref[:, cols].astype(F32)).astype(BF16)
 
     mine = pl.multiple_of((x * 4 + y) * 256, 256)
     k_own = pltpu.make_async_copy(k_ref.at[:, pl.ds(mine, 256)], kbuf.at[pl.ds(0, 128)], a2a_recv.at[0, 0])
@@ -73,7 +82,7 @@
     pl.semaphore_wait(barrier, 19)
 
     def block_copy(kind, source, target, slot):
-        dx, dy = OFFSETS[slot]
+        dx, dy = (Q_OFFSETS if kind == 2 else K_OFFSETS)[slot]
         to = pl.multiple_of((((x + dx) % 4) * 4 + (y + dy) % 4) * 256, 256)
         return remote(
             source.at[:, pl.ds(to, 256)], target.at[pl.ds(slot * 128, 128)],
@@ -92,11 +101,15 @@
     mom_over = remote(mom_ref.at[local, :, pl.ds(row_other, 128)], mom, w_send.at[3], w_recv.at[3], dev(dc=1))
 
     a2a = []
-    for slot in SEND_ORDER[:3]:
-        for kind, source, target in ((0, k_ref, kbuf), (1, gsrc, gbuf)):
-            copy = block_copy(kind, source, target, slot)
-            copy.start()
-            a2a.append(copy)
+
+    def send_group(slots):
+        for slot in slots:
+            for kind, source, target in ((0, k_ref, kbuf), (1, gsrc, gbuf)):
+                copy = block_copy(kind, source, target, slot)
+                copy.start()
+                a2a.append(copy)
+
+    send_group((1, 2, 3, 4))
 
     @pl.when(c == owner)
     def _():
@@ -106,16 +119,7 @@
         mom_over.start()
         mom_in.start()
 
-    for slot in SEND_ORDER[3:]:
-        for kind, source, target in ((0, k_ref, kbuf), (1, gsrc, gbuf)):
-            copy = block_copy(kind, source, target, slot)
-            copy.start()
-            a2a.append(copy)
-    for slot in SEND_ORDER:
-        copy = block_copy(2, q_ref, qbuf, slot)
-        copy.start()
-        a2a.append(copy)
-    q_own.start()
+    send_group(range(5, 16))
 
     for m in range(3):
         @pl.when(c == owner)
@@ -166,19 +170,18 @@
         ).wait_recv()
 
     k_own.wait()
-    slot_wait(0, kbuf, 1)
-    slot_wait(1, gbuf, 1)
-    grad_block(0, True)
-
-    def later(t, carry):
-        for j in range(2):
-            slot = 2 * t + j
-            slot_wait(0, kbuf, slot)
-            slot_wait(1, gbuf, slot)
-        grad_block(t, False)
-        return carry
-
-    lax.fori_loop(1, 8, later, 0)
+    for t in range(8):
+        for slot in (2 * t, 2 * t + 1):
+            if slot > 0:
+                slot_wait(0, kbuf, slot)
+                slot_wait(1, gbuf, slot)
+        if t == 7:
+            for slot in Q_ORDER:
+                copy = block_copy(2, q_ref, qbuf, slot)
+                copy.start()
+                a2a.append(copy)
+            q_own.start()
+        grad_block(t, t == 0)
 
     wo_rows = pl.ds(pl.multiple_of(c * 512, 512), 512)
     wo_in = pltpu.make_async_copy(wout_ref, wout.at[wo_rows], loc_sem.at[4])
@@ -260,30 +263,61 @@
 
     my_cols = pl.ds(pl.multiple_of(y * 256, 256), 256)
     o_copies = []
-    for t in (6, 7, 4, 5, 2, 3, 0, 1):
-        for slot in (2 * t, 2 * t + 1):
-            if slot > 0:
-                slot_wait(2, qbuf, slot)
-        apply_slots(t)
-        for slot in (2 * t, 2 * t + 1):
-            dx, dy = OFFSETS[slot]
-            if dy == 0:
-                obuf[pl.ds(dx * 128, 128), my_cols] = osend[pl.ds(slot * 128, 128), :]
-            else:
-                copy = remote(
-                    osend.at[pl.ds(slot * 128, 128)], obuf.at[pl.ds(dx * 128, 128), my_cols],
-                    os_sem.at[dx, dy], or_sem.at[dx, dy], dev(dy=-dy),
-                )
-                copy.start()
-                o_copies.append(copy)
+
+    def apply_blocks(*blocks):
+        for t in blocks:
+            for slot in (2 * t, 2 * t + 1):
+                if slot > 0:
+                    slot_wait(2, qbuf, slot)
+            apply_slots(t)
+            for slot in (2 * t, 2 * t + 1):
+                dx, dy = Q_OFFSETS[slot]
+                if dy == 0:
+                    obuf[pl.ds(dx * 128, 128), my_cols] = osend[pl.ds(slot * 128, 128), :]
+                else:
+                    copy = remote(
+                        osend.at[pl.ds(slot * 128, 128)], obuf.at[pl.ds(dx * 128, 128), my_cols],
+                        os_sem.at[dx, dy], or_sem.at[dx, dy], dev(dy=-dy),
+                    )
+                    copy.start()
+                    o_copies.append(copy)
+
+    def apply_far(half):
+        def body(i, acc):
+            rows = pl.ds(pl.multiple_of(i * chunk, chunk), chunk)
+            query = jnp.concatenate([qbuf[pl.ds(slot * 128 + half * 64, 64), :] for slot in range(4, 8)], axis=0)
+            pre = dot_nt(query, normed[0, rows, :])
+            gate = dot_nt(query, normed[1, rows, :])
+            hidden = (pre * (0.5 + 0.5 * jnp.tanh(0.5 * pre)) * gate).astype(BF16)
+            return acc + dot_nn(hidden, normed[2, rows, :])
+
+        acc = lax.fori_loop(0, 1024 // chunk, body, jnp.zeros((256, 256), F32))
+        result = (acc * cscale[...]).astype(BF16)
+        obuf[pl.ds(256 + half * 64, 64), my_cols] = result[0:64]
+        for n in (3, 1, 2):
+            rows = pl.ds((4 + n) * 128 + half * 64, 64)
+            osend[rows, :] = result[n * 64 : n * 64 + 64]
+            dy = Q_OFFSETS[4 + n][1]
+            copy = remote(
+                osend.at[rows], obuf.at[pl.ds(256 + half * 64, 64), my_cols],
+                os_sem.at[2 + 2 * half, dy], or_sem.at[2 + 2 * half, dy], dev(dy=-dy),
+            )
+            copy.start()
+            o_copies.append(copy)
+
+    for slot in range(4, 8):
+        slot_wait(2, qbuf, slot)
+    apply_far(0)
+    apply_far(1)
+    apply_blocks(4, 5)
 
     wo_in.wait()
     wo_over.wait_recv()
 
-    def o_wait(dx):
+    def o_wait(dx, rows=128):
         for dy in (1, 2, 3):
             remote(
-                osend.at[pl.ds(0, 128)], obuf.at[pl.ds(dx * 128, 128), pl.ds(0, 256)],
+                osend.at[pl.ds(0, rows)], obuf.at[pl.ds(0, rows), pl.ds(0, 256)],
                 os_sem.at[dx, dy], or_sem.at[dx, dy], dev(1),
             ).wait_recv()
 
@@ -292,27 +326,35 @@
             msend.at[kind, j], mrecv.at[kind, j], ms_sem.at[kind, j], mr_sem.at[kind, j], dev(1 if up else -1)
         )
 
-    def product(first, rows, j):
-        return dot_nn(obuf[pl.ds(first, rows), :], wout[:, pl.ds(pl.multiple_of(j * 512, 512), 512)])
-
-    o_wait(2)
-
-    def far(j, carry):
-        msend[0, j] = product(256, 128, j).astype(BF16)
-        message(0, j, True).start()
-        msend[1, j] = product(256, 128, j + 4).astype(BF16)
-        message(1, j, False).start()
-        return carry
-
-    lax.fori_loop(0, 4, far, 0)
+    def product(first, rows, j, width=512):
+        return dot_nn(obuf[pl.ds(first, rows), :], wout[:, pl.ds(pl.multiple_of(j * width, width), width)])
+
+    def far_message(kind, part):
+        return remote(
+            fsend.at[kind, part], frecv.at[kind, part], fs_sem.at[kind, part], fr_sem.at[kind, part],
+            dev(-1 if kind else 1),
+        )
+
+    for half in (0, 1):
+        o_wait(2 + 2 * half, 64)
+
+        def far(n, carry):
+            j, kind = n // 2, n % 2
+            fsend[kind, 2 * half + j] = product(256 + half * 64, 64, j + 2 * kind, 1024).astype(BF16)
+            far_message(kind, 2 * half + j).start()
+            return carry
+
+        for n in range(4):
+            far(n, 0)
+    apply_blocks(6, 7, 1, 0)
     o_wait(1)
     o_wait(3)
 
     def near(j, carry):
-        msend[2, j] = product(384, 128, j + 4).astype(BF16)
-        message(2, j, True).start()
-        msend[3, j] = product(128, 128, j).astype(BF16)
-        message(3, j, False).start()
+        msend[0, j] = product(384, 128, j + 4).astype(BF16)
+        message(0, j, True).start()
+        msend[1, j] = product(128, 128, j).astype(BF16)
+        message(1, j, False).start()
         return carry
 
     lax.fori_loop(0, 4, near, 0)
@@ -324,16 +366,18 @@
 
     lax.fori_loop(0, 4, relay_part, 0)
 
-    def relay(j, carry):
-        message(0, j, True).wait_recv()
-        msend[4, j] = (stash[0, j] + mrecv[0, j].astype(F32)).astype(BF16)
-        message(4, j, True).start()
-        message(1, j, False).wait_recv()
-        msend[5, j] = (stash[1, j] + mrecv[1, j].astype(F32)).astype(BF16)
-        message(5, j, False).start()
-        return carry
-
-    lax.fori_loop(0, 4, relay, 0)
+    for j in range(4):
+        for kind in (0, 1):
+            if j % 2 == 0:
+                far_message(kind, j // 2).wait_recv()
+                far_message(kind, 2 + j // 2).wait_recv()
+            for half in (0, 1):
+                rows, cols = pl.ds(half * 64, 64), pl.ds((j % 2) * 512, 512)
+                msend[2 + kind, j, rows, :] = (
+                    stash[kind, j, rows, :] + frecv[kind, 2 * half + j // 2, :, cols].astype(F32)
+                ).astype(BF16)
+            message(2 + kind, j, kind == 0).start()
+
     o_wait(0)
 
     def rest(j, carry):
@@ -345,12 +389,12 @@
     def finish(j, carry):
         low = pl.ds(pl.multiple_of(j * 512, 512), 512)
         high = pl.ds(pl.multiple_of(j * 512 + 2048, 512), 512)
+        message(1, j, False).wait_recv()
+        message(0, j, True).wait_recv()
+        message(2, j, True).wait_recv()
+        out_ref[:, low] = (total[j] + mrecv[1, j].astype(F32) + mrecv[2, j].astype(F32)).astype(BF16)
         message(3, j, False).wait_recv()
-        message(2, j, True).wait_recv()
-        message(4, j, True).wait_recv()
-        out_ref[:, low] = (total[j] + mrecv[3, j].astype(F32) + mrecv[4, j].astype(F32)).astype(BF16)
-        message(5, j, False).wait_recv()
-        out_ref[:, high] = (total[j + 4] + mrecv[2, j].astype(F32) + mrecv[5, j].astype(F32)).astype(BF16)
+        out_ref[:, high] = (total[j + 4] + mrecv[0, j].astype(F32) + mrecv[3, j].astype(F32)).astype(BF16)
         return carry
 
     lax.fori_loop(0, 4, finish, 0)
@@ -366,8 +410,10 @@
         mom_over.wait_send()
 
     def drain(j, carry):
-        for kind in range(6):
+        for kind in range(4):
             message(kind, j, kind % 2 == 0).wait_send()
+        for kind in range(2):
+            far_message(kind, j).wait_send()
         return carry
 
     lax.fori_loop(0, 4, drain, 0)
@@ -380,7 +426,7 @@
     dma = pltpu.SemaphoreType.DMA
     return pl.pallas_call(
         functools.partial(kernel, float(tokens) ** (-0.5)),
-        out_shape=jax.ShapeDtypeStruct((128, 4096), BF16),
+        out_shape=pltpu.VMEM((128, 4096), BF16),
         in_specs=[anywhere, anywhere, vmem, vmem, anywhere, anywhere, anywhere],
         out_specs=vmem,
         scratch_shapes=[
@@ -403,14 +449,17 @@
             pltpu.VMEM((1024, 4096), BF16),
             pltpu.VMEM((2, 4, 128, 512), F32),
             pltpu.VMEM((8, 128, 512), F32),
-            pltpu.VMEM((6, 4, 128, 512), BF16),
-            pltpu.VMEM((6, 4, 128, 512), BF16),
+            pltpu.VMEM((4, 4, 128, 512), BF16),
+            pltpu.VMEM((4, 4, 128, 512), BF16),
+            pltpu.VMEM((2, 4, 64, 1024), BF16),
+            pltpu.VMEM((2, 4, 64, 1024), BF16),
             dma((3, 16)), dma((3, 16)), dma((5,)), dma((4,)), dma((4,)), dma((4,)), dma((4,)), dma((3,)), dma((3,)),
-            dma((3,)), dma((3,)), dma((4,)), dma((4,)), dma((4, 4)), dma((4, 4)), dma((6, 4)), dma((6, 4)), dma(()), dma(()),
+            dma((3,)), dma((3,)), dma((4,)), dma((4,)), dma((5, 4)), dma((5, 4)), dma((4, 4)), dma((4, 4)),
+            dma((2, 4)), dma((2, 4)), dma(()), dma(()),
         ],
         compiler_params=pltpu.CompilerParams(collective_id=0, has_side_effects=True, vmem_limit_bytes=62 * 2**20),
         name="ttt_layer",
-    )(query_rows, key_rows, value_rows, token_rates, fast_weights, momentum, out_weight)
+    )(query_rows, key_rows, value_rows, token_rates.T, fast_weights, momentum, out_weight)
 
 
 def solution(mesh):

time: 121 us -> 110 us (0.909)
  the two profiles are of different devices: /device:TPU:1 before, /device:TPU:39 now
where the time goes in v2:
time: 110 us
  Pallas kernels  109 us (99%)
    pallas_call x1, Pallas kernels, shards(): pl.pallas_call(functools.partial(kernel, float(tokens) ** (-0.5)), out_sh...  109 us

profile of v2, /device:TPU:39, one launch (start us, length us, event | category | flops | bytes accessed | tf_op | source)
XLA Modules:
  0.0 110.1 jit_solution(8990772949693972418)
XLA Ops:
  0.0 109.1 %ttt_layer.1 = bf16[128,4096]{1,0:T(8,128)(2,1)S(1)} custom-call(bf16[128,4096]{1,0:T(8,128)(2,1)} %q_ref.1, bf16[128,4096]{1,0:T(8,128)(2,1)} %k_ref.1, bf16[128,4096]{1,0:T(8,128)(2,1)} %v_ref.1, f32[16,128]{1,0:T(8,128)} %bitcast.1, f32[2,3,1024,256]{3,2,1,0:T(8,128)} %fast_ref.1, f32[2,3,1024,256]{3,2,1,0:T(8,128)} %mom_ref.1, bf16[512,4096]{1,0:T(8,128)(2,1)} %wout_ref.1), custom_call_target="tpu_custom_call" | custom-call | tf_op jit(solution)/shard_map/ttt_layer/pallas_call | solution.py:427
  109.1 1.0 copy.9

commit v3 on v2

--- a/solution.py
+++ b/solution.py
@@ -78,6 +78,7 @@
     q_own = pltpu.make_async_copy(q_ref.at[:, pl.ds(mine, 256)], qbuf.at[pl.ds(0, 128)], a2a_recv.at[2, 0])
     k_own.start()
     gbuf[pl.ds(0, 128), :] = gsrc[:, pl.ds(mine, 256)]
+    grad[...] = jnp.zeros_like(grad)
 
     pl.semaphore_wait(barrier, 19)
 
@@ -132,36 +133,20 @@
 
         wb[m] = wf[m].astype(BF16)
 
-    chunk = 512
-
-    def grad_block(t, first):
-        toks = pl.ds(pl.multiple_of(t * 256, 256), 256)
-
-        def body(i, carry):
-            rows = pl.ds(pl.multiple_of(i * chunk, chunk), chunk)
-            keys, gout = kbuf[toks, :], gbuf[toks, :]
-            pre = dot_nt(wb[0, rows, :], keys)
-            gate = dot_nt(wb[1, rows, :], keys)
-            back = dot_nt(wb[2, rows, :], gout)
-            sg = 0.5 + 0.5 * jnp.tanh(0.5 * pre)
-            silu = pre * sg
-            hidden = (silu * gate).astype(BF16)
-            grad_gate = (back * silu).astype(BF16)
-            grad_pre = ((back * gate) * (sg + silu - silu * sg)).astype(BF16)
-            g0 = dot_nn(grad_pre, keys)
-            g1 = dot_nn(grad_gate, keys)
-            g2 = dot_nn(hidden, gout)
-            if first:
-                grad[0, rows, :] = g0
-                grad[1, rows, :] = g1
-                grad[2, rows, :] = g2
-            else:
-                grad[0, rows, :] += g0
-                grad[1, rows, :] += g1
-                grad[2, rows, :] += g2
-            return carry
-
-        lax.fori_loop(0, 1024 // chunk, body, 0)
+    def grad_block(start, size):
+        toks = pl.ds(pl.multiple_of(start, 256), size)
+        keys, gout = kbuf[toks, :], gbuf[toks, :]
+        pre = dot_nt(wb[0], keys)
+        gate = dot_nt(wb[1], keys)
+        back = dot_nt(wb[2], gout)
+        sg = 0.5 + 0.5 * jnp.tanh(0.5 * pre)
+        silu = pre * sg
+        hidden = (silu * gate).astype(BF16)
+        grad_gate = (back * silu).astype(BF16)
+        grad_pre = ((back * gate) * (sg + silu - silu * sg)).astype(BF16)
+        grad[0] += dot_nn(grad_pre, keys)
+        grad[1] += dot_nn(grad_gate, keys)
+        grad[2] += dot_nn(hidden, gout)
 
     def slot_wait(kind, target, slot):
         remote(
@@ -170,18 +155,28 @@
         ).wait_recv()
 
     k_own.wait()
-    for t in range(8):
-        for slot in (2 * t, 2 * t + 1):
-            if slot > 0:
-                slot_wait(0, kbuf, slot)
-                slot_wait(1, gbuf, slot)
-        if t == 7:
-            for slot in Q_ORDER:
-                copy = block_copy(2, q_ref, qbuf, slot)
-                copy.start()
-                a2a.append(copy)
-            q_own.start()
-        grad_block(t, t == 0)
+
+    def block(t, carry):
+        @pl.when(t > 0)
+        def _():
+            slot_wait(0, kbuf, 2 * t)
+            slot_wait(1, gbuf, 2 * t)
+
+        slot_wait(0, kbuf, 2 * t + 1)
+        slot_wait(1, gbuf, 2 * t + 1)
+        grad_block(t * 256, 256)
+        return carry
+
+    lax.fori_loop(0, 6, block, 0)
+    for slot in range(12, 16):
+        slot_wait(0, kbuf, slot)
+        slot_wait(1, gbuf, slot)
+    for slot in Q_ORDER:
+        copy = block_copy(2, q_ref, qbuf, slot)
+        copy.start()
+        a2a.append(copy)
+    q_own.start()
+    grad_block(1536, 512)
 
     wo_rows = pl.ds(pl.multiple_of(c * 512, 512), 512)
     wo_in = pltpu.make_async_copy(wout_ref, wout.at[wo_rows], loc_sem.at[4])
@@ -195,13 +190,28 @@
         copy.start()
         core_copies.append(copy)
     z_copies = []
-    for n, dz in enumerate((2, 1, 3)):
-        rows = pl.ds(pl.multiple_of(c * 512 + ((z + dz) % 4) * 128, 128), 128)
-        core_copies[n].wait_recv()
-        zsend[n] = (grad[:, rows, :] + crecv[n].astype(F32)).astype(BF16)
+
+    def piece(n, dz, part):
+        rows = pl.ds(pl.multiple_of(c * 512 + ((z + dz) % 4) * 128 + part * 64, 64), 64)
+        return grad[:, rows, :] + crecv[n, :, pl.ds(part * 64, 64), :].astype(F32)
+
+    def z_send(n, value, dz):
+        zsend[n] = value.astype(BF16)
         copy = remote(zsend.at[n], zrecv.at[n], zs_sem.at[n], zr_sem.at[n], dev(dz=dz))
         copy.start()
         z_copies.append(copy)
+
+    core_copies[0].wait_recv()
+    z_send(0, piece(0, 2, 0), 1)
+    z_send(1, piece(0, 2, 1), -1)
+    core_copies[1].wait_recv()
+    z_send(2, piece(1, 1, 1), 1)
+    core_copies[2].wait_recv()
+    z_send(3, piece(2, 3, 0), -1)
+    z_copies[0].wait_recv()
+    z_send(4, piece(1, 1, 0) + zrecv[0].astype(F32), 1)
+    z_copies[1].wait_recv()
+    z_send(5, piece(2, 3, 1) + zrecv[1].astype(F32), -1)
     wo_in.start()
     wo_over.start()
     core_copies[3].wait_recv()
@@ -219,27 +229,45 @@
     grad[:, own, :] = base
     row_old = jnp.sqrt(jnp.sum(jnp.square(wf[0:2, own, :]), axis=2, keepdims=True))
     column_old = jnp.sqrt(jnp.sum(jnp.square(wf[2]), axis=0, keepdims=True))
-    for n in range(3):
+    for n in range(2, 6):
         z_copies[n].wait_recv()
-    updated = grad[:, own, :] - (zrecv[0].astype(F32) + zrecv[1].astype(F32) + zrecv[2].astype(F32))
+    others = jnp.concatenate(
+        [zrecv[4].astype(F32) + zrecv[3].astype(F32), zrecv[2].astype(F32) + zrecv[5].astype(F32)], axis=1
+    )
+    updated = grad[:, own, :] - others
     row_new = jnp.sum(jnp.square(updated[0:2]), axis=2, keepdims=True)
     normed[0:2, own, :] = (updated[0:2] * row_old / jnp.sqrt(row_new + 1e-06)).astype(BF16)
     normed[2, own, :] = updated[2].astype(BF16)
 
+    def half_rows(dz, part):
+        return pl.ds(pl.multiple_of(c * 512 + ((z + dz) % 4) * 128 + part * 64, 64), 64)
+
     n_copies, p_copies = [], []
-    for n, dz in enumerate((2, 1, 3)):
-        copy = remote(normed.at[:, own], normed.at[:, own], ns_sem.at[n], nr_sem.at[n], dev(dz=dz))
+
+    def n_send(n, rows, dz):
+        copy = remote(normed.at[:, rows], normed.at[:, rows], ns_sem.at[n], nr_sem.at[n], dev(dz=dz))
         copy.start()
         n_copies.append(copy)
-    copy = remote(normed.at[:, own], normed.at[:, own], ps_sem.at[3], pr_sem.at[3], dev(dc=1))
-    copy.start()
-    p_copies.append(copy)
-    for n, dz in ((1, 1), (2, 3), (0, 2)):
-        n_copies[n].wait_recv()
-        rows = pl.ds(pl.multiple_of(c * 512 + ((z - dz) % 4) * 128, 128), 128)
+
+    def p_send(n, rows):
         copy = remote(normed.at[:, rows], normed.at[:, rows], ps_sem.at[n], pr_sem.at[n], dev(dc=1))
         copy.start()
         p_copies.append(copy)
+
+    n_send(0, half_rows(0, 0), 1)
+    n_send(1, half_rows(0, 1), -1)
+    n_send(2, half_rows(0, 1), 1)
+    n_send(3, half_rows(0, 0), -1)
+    p_send(6, own)
+    n_copies[0].wait_recv()
+    n_send(4, half_rows(-1, 0), 1)
+    p_send(0, half_rows(-1, 0))
+    n_copies[1].wait_recv()
+    n_send(5, half_rows(1, 1), -1)
+    p_send(1, half_rows(1, 1))
+    for n, dz, part in ((2, -1, 1), (3, 1, 0), (4, 2, 0), (5, 2, 1)):
+        n_copies[n].wait_recv()
+        p_send(n, half_rows(dz, part))
     for copy in p_copies:
         copy.wait_recv()
     column_new = jnp.sum(jnp.square(normed[2].astype(F32)), axis=0, keepdims=True)
@@ -247,52 +275,39 @@
 
     q_own.wait()
 
-    def apply_slots(t):
-        toks = pl.ds(t * 256, 256)
-
-        def body(i, acc):
-            rows = pl.ds(pl.multiple_of(i * chunk, chunk), chunk)
-            query = qbuf[toks, :]
+    def applied(query):
+        hidden = []
+        for i in range(4):
+            rows = pl.ds(i * 256, 256)
             pre = dot_nt(query, normed[0, rows, :])
             gate = dot_nt(query, normed[1, rows, :])
-            hidden = (pre * (0.5 + 0.5 * jnp.tanh(0.5 * pre)) * gate).astype(BF16)
-            return acc + dot_nn(hidden, normed[2, rows, :])
-
-        acc = lax.fori_loop(0, 1024 // chunk, body, jnp.zeros((256, 256), F32))
-        osend[toks, :] = (acc * cscale[...]).astype(BF16)
+            hidden.append((pre * (0.5 + 0.5 * jnp.tanh(0.5 * pre)) * gate).astype(BF16))
+        return (dot_nn(jnp.concatenate(hidden, axis=1), normed[2]) * cscale[...]).astype(BF16)
 
     my_cols = pl.ds(pl.multiple_of(y * 256, 256), 256)
     o_copies = []
 
-    def apply_blocks(*blocks):
-        for t in blocks:
-            for slot in (2 * t, 2 * t + 1):
-                if slot > 0:
-                    slot_wait(2, qbuf, slot)
-            apply_slots(t)
-            for slot in (2 * t, 2 * t + 1):
-                dx, dy = Q_OFFSETS[slot]
-                if dy == 0:
-                    obuf[pl.ds(dx * 128, 128), my_cols] = osend[pl.ds(slot * 128, 128), :]
-                else:
-                    copy = remote(
-                        osend.at[pl.ds(slot * 128, 128)], obuf.at[pl.ds(dx * 128, 128), my_cols],
-                        os_sem.at[dx, dy], or_sem.at[dx, dy], dev(dy=-dy),
-                    )
-                    copy.start()
-                    o_copies.append(copy)
+    def apply_group(first):
+        for slot in range(first, first + 4):
+            if slot > 0:
+                slot_wait(2, qbuf, slot)
+        osend[pl.ds(first * 128, 512), :] = applied(qbuf[pl.ds(first * 128, 512), :])
+        for slot in range(first, first + 4):
+            dx, dy = Q_OFFSETS[slot]
+            if dy == 0:
+                obuf[pl.ds(dx * 128, 128), my_cols] = osend[pl.ds(slot * 128, 128), :]
+            else:
+                copy = remote(
+                    osend.at[pl.ds(slot * 128, 128)], obuf.at[pl.ds(dx * 128, 128), my_cols],
+                    os_sem.at[dx, dy], or_sem.at[dx, dy], dev(dy=-dy),
+                )
+                copy.start()
+                o_copies.append(copy)
 
     def apply_far(half):
-        def body(i, acc):
-            rows = pl.ds(pl.multiple_of(i * chunk, chunk), chunk)
-            query = jnp.concatenate([qbuf[pl.ds(slot * 128 + half * 64, 64), :] for slot in range(4, 8)], axis=0)
-            pre = dot_nt(query, normed[0, rows, :])
-            gate = dot_nt(query, normed[1, rows, :])
-            hidden = (pre * (0.5 + 0.5 * jnp.tanh(0.5 * pre)) * gate).astype(BF16)
-            return acc + dot_nn(hidden, normed[2, rows, :])
-
-        acc = lax.fori_loop(0, 1024 // chunk, body, jnp.zeros((256, 256), F32))
-        result = (acc * cscale[...]).astype(BF16)
+        result = applied(
+            jnp.concatenate([qbuf[pl.ds(slot * 128 + half * 64, 64), :] for slot in range(4, 8)], axis=0)
+        )
         obuf[pl.ds(256 + half * 64, 64), my_cols] = result[0:64]
         for n in (3, 1, 2):
             rows = pl.ds((4 + n) * 128 + half * 64, 64)
@@ -309,7 +324,7 @@
         slot_wait(2, qbuf, slot)
     apply_far(0)
     apply_far(1)
-    apply_blocks(4, 5)
+    apply_group(8)
 
     wo_in.wait()
     wo_over.wait_recv()
@@ -346,7 +361,8 @@
 
         for n in range(4):
             far(n, 0)
-    apply_blocks(6, 7, 1, 0)
+    apply_group(12)
+    apply_group(0)
     o_wait(1)
     o_wait(3)
 
@@ -440,8 +456,8 @@
             pltpu.VMEM((3, 1024, 256), F32),
             pltpu.VMEM((4, 3, 128, 256), BF16),
             pltpu.VMEM((4, 3, 128, 256), BF16),
-            pltpu.VMEM((3, 3, 128, 256), BF16),
-            pltpu.VMEM((3, 3, 128, 256), BF16),
+            pltpu.VMEM((6, 3, 64, 256), BF16),
+            pltpu.VMEM((6, 3, 64, 256), BF16),
             pltpu.VMEM((3, 1024, 256), BF16),
             pltpu.VMEM((1, 256), F32),
             pltpu.VMEM((2048, 256), BF16),
@@ -453,8 +469,8 @@
             pltpu.VMEM((4, 4, 128, 512), BF16),
             pltpu.VMEM((2, 4, 64, 1024), BF16),
             pltpu.VMEM((2, 4, 64, 1024), BF16),
-            dma((3, 16)), dma((3, 16)), dma((5,)), dma((4,)), dma((4,)), dma((4,)), dma((4,)), dma((3,)), dma((3,)),
-            dma((3,)), dma((3,)), dma((4,)), dma((4,)), dma((5, 4)), dma((5, 4)), dma((4, 4)), dma((4, 4)),
+            dma((3, 16)), dma((3, 16)), dma((5,)), dma((4,)), dma((4,)), dma((4,)), dma((4,)), dma((6,)), dma((6,)),
+            dma((6,)), dma((6,)), dma((7,)), dma((7,)), dma((5, 4)), dma((5, 4)), dma((4, 4)), dma((4, 4)),
             dma((2, 4)), dma((2, 4)), dma(()), dma(()),
         ],
         compiler_params=pltpu.CompilerParams(collective_id=0, has_side_effects=True, vmem_limit_bytes=62 * 2**20),

time: 110 us -> 105 us (0.955)
  the two profiles are of different devices: /device:TPU:39 before, /device:TPU:1 now
where the time goes in v3:
time: 105 us; the launch traced here: 104 us
  Pallas kernels  104 us (99%)
    pallas_call x1, Pallas kernels, shards(): pl.pallas_call(functools.partial(kernel, float(tokens) ** (-0.5)), out_sh...  104 us

profile of v3, /device:TPU:1, one launch (start us, length us, event | category | flops | bytes accessed | tf_op | source)
XLA Modules:
  0.0 104.5 jit_solution(2230049729969646071)
XLA Ops:
  0.0 103.5 %ttt_layer.1 = bf16[128,4096]{1,0:T(8,128)(2,1)S(1)} custom-call(bf16[128,4096]{1,0:T(8,128)(2,1)} %q_ref.1, bf16[128,4096]{1,0:T(8,128)(2,1)} %k_ref.1, bf16[128,4096]{1,0:T(8,128)(2,1)} %v_ref.1, f32[16,128]{1,0:T(8,128)} %bitcast.1, f32[2,3,1024,256]{3,2,1,0:T(8,128)} %fast_ref.1, f32[2,3,1024,256]{3,2,1,0:T(8,128)} %mom_ref.1, bf16[512,4096]{1,0:T(8,128)(2,1)} %wout_ref.1), custom_call_target="tpu_custom_call" | custom-call | tf_op jit(solution)/shard_map/ttt_layer/pallas_call | solution.py:443
  103.5 1.0 copy.9

commit v4 on v3

--- a/solution.py
+++ b/solution.py
@@ -41,7 +41,7 @@
     rate_scale,
     q_ref, k_ref, v_ref, rates_ref, fast_ref, mom_ref, wout_ref,
     out_ref,
-    gsrc, kbuf, gbuf, qbuf, wf, wb, mom, grad,
+    vbuf, gsrc, kbuf, gbuf, qbuf, wf, wb, mom, grad,
     csend, crecv, zsend, zrecv, normed, cscale,
     osend, obuf, wout, stash, total, msend, mrecv, fsend, frecv,
     a2a_send, a2a_recv, loc_sem, w_send, w_recv, cs_sem, cr_sem, zs_sem, zr_sem,
@@ -68,17 +68,12 @@
         pl.semaphore_signal(barrier, inc=1, device_id=dev(dz=dz), device_id_type=MESH)
     pl.semaphore_signal(barrier, inc=1, device_id=dev(dc=1), device_id_type=MESH)
 
-    scaled = -(rates_ref[...].T * rate_scale)
-    for h in range(16):
-        cols = pl.ds(h * 256, 256)
-        gsrc[:, cols] = (scaled[:, h : h + 1] * v_ref[:, cols].astype(F32)).astype(BF16)
-
+    v_in = pltpu.make_async_copy(v_ref, vbuf, loc_sem.at[5])
+    v_in.start()
     mine = pl.multiple_of((x * 4 + y) * 256, 256)
     k_own = pltpu.make_async_copy(k_ref.at[:, pl.ds(mine, 256)], kbuf.at[pl.ds(0, 128)], a2a_recv.at[0, 0])
     q_own = pltpu.make_async_copy(q_ref.at[:, pl.ds(mine, 256)], qbuf.at[pl.ds(0, 128)], a2a_recv.at[2, 0])
     k_own.start()
-    gbuf[pl.ds(0, 128), :] = gsrc[:, pl.ds(mine, 256)]
-    grad[...] = jnp.zeros_like(grad)
 
     pl.semaphore_wait(barrier, 19)
 
@@ -103,24 +98,34 @@
 
     a2a = []
 
-    def send_group(slots):
+    def send(kind, source, target, slots):
         for slot in slots:
-            for kind, source, target in ((0, k_ref, kbuf), (1, gsrc, gbuf)):
-                copy = block_copy(kind, source, target, slot)
-                copy.start()
-                a2a.append(copy)
-
-    send_group((1, 2, 3, 4))
+            copy = block_copy(kind, source, target, slot)
+            copy.start()
+            a2a.append(copy)
+
+    send(0, k_ref, kbuf, range(1, 5))
 
     @pl.when(c == owner)
     def _():
         for m in range(3):
+            weights_in(m).start()
+        mom_in.start()
+        for m in range(3):
             weights_over(m).start()
-            weights_in(m).start()
         mom_over.start()
-        mom_in.start()
-
-    send_group(range(5, 16))
+
+    scaled = -(rates_ref[...].T * rate_scale)
+    v_in.wait()
+    for h in range(16):
+        cols = pl.ds(h * 256, 256)
+        gsrc[:, cols] = (scaled[:, h : h + 1] * vbuf[:, cols].astype(F32)).astype(BF16)
+    gbuf[pl.ds(0, 128), :] = gsrc[:, pl.ds(mine, 256)]
+    send(1, gsrc, gbuf, range(1, 5))
+    for slot in range(5, 16):
+        send(0, k_ref, kbuf, (slot,))
+        send(1, gsrc, gbuf, (slot,))
+    grad[...] = jnp.zeros_like(grad)
 
     for m in range(3):
         @pl.when(c == owner)
@@ -171,25 +176,36 @@
     for slot in range(12, 16):
         slot_wait(0, kbuf, slot)
         slot_wait(1, gbuf, slot)
-    for slot in Q_ORDER:
-        copy = block_copy(2, q_ref, qbuf, slot)
-        copy.start()
-        a2a.append(copy)
+    send(2, q_ref, qbuf, Q_ORDER)
     q_own.start()
-    grad_block(1536, 512)
-
     wo_rows = pl.ds(pl.multiple_of(c * 512, 512), 512)
     wo_in = pltpu.make_async_copy(wout_ref, wout.at[wo_rows], loc_sem.at[4])
     wo_over = remote(wout_ref, wout.at[wo_rows], wo_send, wo_recv, dev(dc=1))
 
-    core_copies = []
-    for n, dz in enumerate((2, 1, 3, 0)):
-        rows = pl.ds(pl.multiple_of((1 - c) * 512 + ((z + dz) % 4) * 128, 128), 128)
-        csend[n] = grad[:, rows, :].astype(BF16)
+    core_copies, z_copies = [], []
+
+    def last_piece(n, dz):
+        kept = pl.ds(pl.multiple_of(c * 512 + ((z + dz) % 4) * 128, 128), 128)
+        given = pl.ds(pl.multiple_of((1 - c) * 512 + ((z + dz) % 4) * 128, 128), 128)
+        keys, gout = kbuf[pl.ds(1536, 512), :], gbuf[pl.ds(1536, 512), :]
+
+        def both(m):
+            return jnp.concatenate([wb[m, given, :], wb[m, kept, :]], axis=0)
+
+        pre = dot_nt(both(0), keys)
+        gate = dot_nt(both(1), keys)
+        back = dot_nt(both(2), gout)
+        sg = 0.5 + 0.5 * jnp.tanh(0.5 * pre)
+        silu = pre * sg
+        hidden = (silu * gate).astype(BF16)
+        grad_gate = (back * silu).astype(BF16)
+        grad_pre = ((back * gate) * (sg + silu - silu * sg)).astype(BF16)
+        for m, sums in ((0, dot_nn(grad_pre, keys)), (1, dot_nn(grad_gate, keys)), (2, dot_nn(hidden, gout))):
+            csend[n, m] = (grad[m, given, :] + sums[:128]).astype(BF16)
+            grad[m, kept, :] += sums[128:]
         copy = remote(csend.at[n], crecv.at[n], cs_sem.at[n], cr_sem.at[n], dev(dc=1))
         copy.start()
         core_copies.append(copy)
-    z_copies = []
 
     def piece(n, dz, part):
         rows = pl.ds(pl.multiple_of(c * 512 + ((z + dz) % 4) * 128 + part * 64, 64), 64)
@@ -201,11 +217,15 @@
         copy.start()
         z_copies.append(copy)
 
+    last_piece(0, 2)
+    last_piece(1, 1)
     core_copies[0].wait_recv()
     z_send(0, piece(0, 2, 0), 1)
     z_send(1, piece(0, 2, 1), -1)
+    last_piece(2, 3)
     core_copies[1].wait_recv()
     z_send(2, piece(1, 1, 1), 1)
+    last_piece(3, 0)
     core_copies[2].wait_recv()
     z_send(3, piece(2, 3, 0), -1)
     z_copies[0].wait_recv()
@@ -443,9 +463,10 @@
     return pl.pallas_call(
         functools.partial(kernel, float(tokens) ** (-0.5)),
         out_shape=pltpu.VMEM((128, 4096), BF16),
-        in_specs=[anywhere, anywhere, vmem, vmem, anywhere, anywhere, anywhere],
+        in_specs=[anywhere, anywhere, anywhere, vmem, anywhere, anywhere, anywhere],
         out_specs=vmem,
         scratch_shapes=[
+            pltpu.VMEM((128, 4096), BF16),
             pltpu.VMEM((128, 4096), BF16),
             pltpu.VMEM((2048, 256), BF16),
             pltpu.VMEM((2048, 256), BF16),
@@ -469,7 +490,7 @@
             pltpu.VMEM((4, 4, 128, 512), BF16),
             pltpu.VMEM((2, 4, 64, 1024), BF16),
             pltpu.VMEM((2, 4, 64, 1024), BF16),
-            dma((3, 16)), dma((3, 16)), dma((5,)), dma((4,)), dma((4,)), dma((4,)), dma((4,)), dma((6,)), dma((6,)),
+            dma((3, 16)), dma((3, 16)), dma((6,)), dma((4,)), dma((4,)), dma((4,)), dma((4,)), dma((6,)), dma((6,)),
             dma((6,)), dma((6,)), dma((7,)), dma((7,)), dma((5, 4)), dma((5, 4)), dma((4, 4)), dma((4, 4)),
             dma((2, 4)), dma((2, 4)), dma(()), dma(()),
         ],

time: 105 us -> 103 us (0.981)
  Pallas kernels: 104 us -> 101 us
    pallas_call x1, Pallas kernels: 104 us -> 101 us  [shards(): pl.pallas_call(functools.partial(kernel, float(tokens) ** (-0.5)), out_sh...]
where the time goes in v4:
time: 103 us; the launch traced here: 102 us
  Pallas kernels  101 us (98%)
    pallas_call x1, Pallas kernels, shards(): pl.pallas_call(functools.partial(kernel, float(tokens) ** (-0.5)), out_sh...  101 us

profile of v4, /device:TPU:1, one launch (start us, length us, event | category | flops | bytes accessed | tf_op | source)
XLA Modules:
  0.0 102.4 jit_solution(13722590359568673044)
XLA Ops:
  0.0 101.4 %ttt_layer.1 = bf16[128,4096]{1,0:T(8,128)(2,1)S(1)} custom-call(bf16[128,4096]{1,0:T(8,128)(2,1)} %q_ref.1, bf16[128,4096]{1,0:T(8,128)(2,1)} %k_ref.1, bf16[128,4096]{1,0:T(8,128)(2,1)} %v_ref.1, f32[16,128]{1,0:T(8,128)} %bitcast.1, f32[2,3,1024,256]{3,2,1,0:T(8,128)} %fast_ref.1, f32[2,3,1024,256]{3,2,1,0:T(8,128)} %mom_ref.1, bf16[512,4096]{1,0:T(8,128)(2,1)} %wout_ref.1), custom_call_target="tpu_custom_call" | custom-call | tf_op jit(solution)/shard_map/ttt_layer/pallas_call | solution.py:463
  101.4 1.0 copy.9

commit v5 on v4

--- a/solution.py
+++ b/solution.py
@@ -207,31 +207,40 @@
         copy.start()
         core_copies.append(copy)
 
-    def piece(n, dz, part):
+    order = (2, 0, 1)
+
+    def piece(n, dz, part, m):
         rows = pl.ds(pl.multiple_of(c * 512 + ((z + dz) % 4) * 128 + part * 64, 64), 64)
-        return grad[:, rows, :] + crecv[n, :, pl.ds(part * 64, 64), :].astype(F32)
-
-    def z_send(n, value, dz):
-        zsend[n] = value.astype(BF16)
-        copy = remote(zsend.at[n], zrecv.at[n], zs_sem.at[n], zr_sem.at[n], dev(dz=dz))
+        return grad[m, rows, :] + crecv[n, m, pl.ds(part * 64, 64), :].astype(F32)
+
+    def z_copy(n, m, dz):
+        return remote(zsend.at[n, m], zrecv.at[n, m], zs_sem.at[n, m], zr_sem.at[n, m], dev(dz=dz))
+
+    def z_send(n, m, value, dz):
+        zsend[n, m] = value.astype(BF16)
+        copy = z_copy(n, m, dz)
         copy.start()
         z_copies.append(copy)
 
     last_piece(0, 2)
     last_piece(1, 1)
     core_copies[0].wait_recv()
-    z_send(0, piece(0, 2, 0), 1)
-    z_send(1, piece(0, 2, 1), -1)
+    for m in order:
+        z_send(0, m, piece(0, 2, 0, m), 1)
+        z_send(1, m, piece(0, 2, 1, m), -1)
     last_piece(2, 3)
     core_copies[1].wait_recv()
-    z_send(2, piece(1, 1, 1), 1)
+    for m in order:
+        z_send(2, m, piece(1, 1, 1, m), 1)
     last_piece(3, 0)
     core_copies[2].wait_recv()
-    z_send(3, piece(2, 3, 0), -1)
-    z_copies[0].wait_recv()
-    z_send(4, piece(1, 1, 0) + zrecv[0].astype(F32), 1)
-    z_copies[1].wait_recv()
-    z_send(5, piece(2, 3, 1) + zrecv[1].astype(F32), -1)
+    for m in order:
+        z_send(3, m, piece(2, 3, 0, m), -1)
+    for m in order:
+        z_copy(0, m, 1).wait_recv()
+        z_send(4, m, piece(1, 1, 0, m) + zrecv[0, m].astype(F32), 1)
+        z_copy(1, m, -1).wait_recv()
+        z_send(5, m, piece(2, 3, 1, m) + zrecv[1, m].astype(F32), -1)
     wo_in.start()
     wo_over.start()
     core_copies[3].wait_recv()
@@ -249,45 +258,48 @@
     grad[:, own, :] = base
     row_old = jnp.sqrt(jnp.sum(jnp.square(wf[0:2, own, :]), axis=2, keepdims=True))
     column_old = jnp.sqrt(jnp.sum(jnp.square(wf[2]), axis=0, keepdims=True))
-    for n in range(2, 6):
-        z_copies[n].wait_recv()
-    others = jnp.concatenate(
-        [zrecv[4].astype(F32) + zrecv[3].astype(F32), zrecv[2].astype(F32) + zrecv[5].astype(F32)], axis=1
-    )
-    updated = grad[:, own, :] - others
-    row_new = jnp.sum(jnp.square(updated[0:2]), axis=2, keepdims=True)
-    normed[0:2, own, :] = (updated[0:2] * row_old / jnp.sqrt(row_new + 1e-06)).astype(BF16)
-    normed[2, own, :] = updated[2].astype(BF16)
-
     def half_rows(dz, part):
         return pl.ds(pl.multiple_of(c * 512 + ((z + dz) % 4) * 128 + part * 64, 64), 64)
 
-    n_copies, p_copies = [], []
-
-    def n_send(n, rows, dz):
-        copy = remote(normed.at[:, rows], normed.at[:, rows], ns_sem.at[n], nr_sem.at[n], dev(dz=dz))
-        copy.start()
-        n_copies.append(copy)
-
-    def p_send(n, rows):
-        copy = remote(normed.at[:, rows], normed.at[:, rows], ps_sem.at[n], pr_sem.at[n], dev(dc=1))
+    n_copies, p_copies = {}, []
+
+    def n_send(n, m, rows, dz):
+        n_copies[n, m] = remote(normed.at[m, rows], normed.at[m, rows], ns_sem.at[n, m], nr_sem.at[n, m], dev(dz=dz))
+        n_copies[n, m].start()
+
+    def p_send(n, m, rows):
+        copy = remote(normed.at[m, rows], normed.at[m, rows], ps_sem.at[n, m], pr_sem.at[n, m], dev(dc=1))
         copy.start()
         p_copies.append(copy)
 
-    n_send(0, half_rows(0, 0), 1)
-    n_send(1, half_rows(0, 1), -1)
-    n_send(2, half_rows(0, 1), 1)
-    n_send(3, half_rows(0, 0), -1)
-    p_send(6, own)
-    n_copies[0].wait_recv()
-    n_send(4, half_rows(-1, 0), 1)
-    p_send(0, half_rows(-1, 0))
-    n_copies[1].wait_recv()
-    n_send(5, half_rows(1, 1), -1)
-    p_send(1, half_rows(1, 1))
-    for n, dz, part in ((2, -1, 1), (3, 1, 0), (4, 2, 0), (5, 2, 1)):
-        n_copies[n].wait_recv()
-        p_send(n, half_rows(dz, part))
+    for m in order:
+        for n in range(2, 6):
+            z_copy(n, m, 1).wait_recv()
+        others = jnp.concatenate(
+            [zrecv[4, m].astype(F32) + zrecv[3, m].astype(F32), zrecv[2, m].astype(F32) + zrecv[5, m].astype(F32)], axis=0
+        )
+        updated = grad[m, own, :] - others
+        if m < 2:
+            row_new = jnp.sum(jnp.square(updated), axis=1, keepdims=True)
+            updated = updated * row_old[m] / jnp.sqrt(row_new + 1e-06)
+        normed[m, own, :] = updated.astype(BF16)
+        n_send(0, m, half_rows(0, 0), 1)
+        n_send(1, m, half_rows(0, 1), -1)
+        n_send(2, m, half_rows(0, 1), 1)
+        n_send(3, m, half_rows(0, 0), -1)
+        p_send(6, m, own)
+    for m in order:
+        n_copies[0, m].wait_recv()
+        n_send(4, m, half_rows(-1, 0), 1)
+        p_send(0, m, half_rows(-1, 0))
+        n_copies[1, m].wait_recv()
+        n_send(5, m, half_rows(1, 1), -1)
+        p_send(1, m, half_rows(1, 1))
+    for pair in (((2, -1, 1), (3, 1, 0)), ((4, 2, 0), (5, 2, 1))):
+        for m in order:
+            for n, dz, part in pair:
+                n_copies[n, m].wait_recv()
+                p_send(n, m, half_rows(dz, part))
     for copy in p_copies:
         copy.wait_recv()
     column_new = jnp.sum(jnp.square(normed[2].astype(F32)), axis=0, keepdims=True)
@@ -345,6 +357,7 @@
     apply_far(0)
     apply_far(1)
     apply_group(8)
+    apply_group(12)
 
     wo_in.wait()
     wo_over.wait_recv()
@@ -361,8 +374,8 @@
             msend.at[kind, j], mrecv.at[kind, j], ms_sem.at[kind, j], mr_sem.at[kind, j], dev(1 if up else -1)
         )
 
-    def product(first, rows, j, width=512):
-        return dot_nn(obuf[pl.ds(first, rows), :], wout[:, pl.ds(pl.multiple_of(j * width, width), width)])
+    def product(first, rows, j):
+        return dot_nn(obuf[pl.ds(first, rows), :], wout[:, pl.ds(pl.multiple_of(j * 512, 512), 512)])
 
     def far_message(kind, part):
         return remote(
@@ -373,16 +386,13 @@
     for half in (0, 1):
         o_wait(2 + 2 * half, 64)
 
-        def far(n, carry):
-            j, kind = n // 2, n % 2
-            fsend[kind, 2 * half + j] = product(256 + half * 64, 64, j + 2 * kind, 1024).astype(BF16)
-            far_message(kind, 2 * half + j).start()
+        def far(j, carry):
+            for kind in (0, 1):
+                fsend[kind, 4 * half + j] = product(256 + half * 64, 64, j + 4 * kind).astype(BF16)
+                far_message(kind, 4 * half + j).start()
             return carry
 
-        for n in range(4):
-            far(n, 0)
-    apply_group(12)
-    apply_group(0)
+        lax.fori_loop(0, 4, far, 0)
     o_wait(1)
     o_wait(3)
 
@@ -395,6 +405,7 @@
 
     lax.fori_loop(0, 4, near, 0)
 
+    apply_group(0)
     def relay_part(j, carry):
         stash[0, j] = product(384, 128, j)
         stash[1, j] = product(128, 128, j + 4)
@@ -404,13 +415,11 @@
 
     for j in range(4):
         for kind in (0, 1):
-            if j % 2 == 0:
-                far_message(kind, j // 2).wait_recv()
-                far_message(kind, 2 + j // 2).wait_recv()
             for half in (0, 1):
-                rows, cols = pl.ds(half * 64, 64), pl.ds((j % 2) * 512, 512)
+                far_message(kind, 4 * half + j).wait_recv()
+                rows = pl.ds(half * 64, 64)
                 msend[2 + kind, j, rows, :] = (
-                    stash[kind, j, rows, :] + frecv[kind, 2 * half + j // 2, :, cols].astype(F32)
+                    stash[kind, j, rows, :] + frecv[kind, 4 * half + j].astype(F32)
                 ).astype(BF16)
             message(2 + kind, j, kind == 0).start()
 
@@ -435,7 +444,7 @@
 
     lax.fori_loop(0, 4, finish, 0)
 
-    for copy in a2a + core_copies + z_copies + n_copies + p_copies + o_copies:
+    for copy in a2a + core_copies + z_copies + list(n_copies.values()) + p_copies + o_copies:
         copy.wait_send()
     wo_over.wait_send()
 
@@ -450,6 +459,7 @@
             message(kind, j, kind % 2 == 0).wait_send()
         for kind in range(2):
             far_message(kind, j).wait_send()
+            far_message(kind, 4 + j).wait_send()
         return carry
 
     lax.fori_loop(0, 4, drain, 0)
@@ -488,11 +498,11 @@
             pltpu.VMEM((8, 128, 512), F32),
             pltpu.VMEM((4, 4, 128, 512), BF16),
             pltpu.VMEM((4, 4, 128, 512), BF16),
-            pltpu.VMEM((2, 4, 64, 1024), BF16),
-            pltpu.VMEM((2, 4, 64, 1024), BF16),
-            dma((3, 16)), dma((3, 16)), dma((6,)), dma((4,)), dma((4,)), dma((4,)), dma((4,)), dma((6,)), dma((6,)),
-            dma((6,)), dma((6,)), dma((7,)), dma((7,)), dma((5, 4)), dma((5, 4)), dma((4, 4)), dma((4, 4)),
-            dma((2, 4)), dma((2, 4)), dma(()), dma(()),
+            pltpu.VMEM((2, 8, 64, 512), BF16),
+            pltpu.VMEM((2, 8, 64, 512), BF16),
+            dma((3, 16)), dma((3, 16)), dma((6,)), dma((4,)), dma((4,)), dma((4,)), dma((4,)), dma((6, 3)), dma((6, 3)),
+            dma((6, 3)), dma((6, 3)), dma((7, 3)), dma((7, 3)), dma((5, 4)), dma((5, 4)), dma((4, 4)), dma((4, 4)),
+            dma((2, 8)), dma((2, 8)), dma(()), dma(()),
         ],
         compiler_params=pltpu.CompilerParams(collective_id=0, has_side_effects=True, vmem_limit_bytes=62 * 2**20),
         name="ttt_layer",

time: 103 us -> 102 us (level)
  no operation moved by 1% of the time
where the time goes in v5:
time: 102 us
  Pallas kernels  101 us (99%)
    pallas_call x1, Pallas kernels, shards(): pl.pallas_call(functools.partial(kernel, float(tokens) ** (-0.5)), out_sh...  101 us

profile of v5, /device:TPU:1, one launch (start us, length us, event | category | flops | bytes accessed | tf_op | source)
XLA Modules:
  0.0 101.8 jit_solution(2957151083578085570)
XLA Ops:
  0.0 100.9 %ttt_layer.1 = bf16[128,4096]{1,0:T(8,128)(2,1)S(1)} custom-call(bf16[128,4096]{1,0:T(8,128)(2,1)} %q_ref.1, bf16[128,4096]{1,0:T(8,128)(2,1)} %k_ref.1, bf16[128,4096]{1,0:T(8,128)(2,1)} %v_ref.1, f32[16,128]{1,0:T(8,128)} %bitcast.1, f32[2,3,1024,256]{3,2,1,0:T(8,128)} %fast_ref.1, f32[2,3,1024,256]{3,2,1,0:T(8,128)} %mom_ref.1, bf16[512,4096]{1,0:T(8,128)(2,1)} %wout_ref.1), custom_call_target="tpu_custom_call" | custom-call | tf_op jit(solution)/shard_map/ttt_layer/pallas_call | solution.py:473
  100.9 1.0 copy.9
